TPU v7x, 256 devices: a whole 4x4x8 slice. The times are simulated.
256 devices in a mesh: prow: 8 (over z), pcol: 32 (over y, x, core).
Axes of the slice: x: 4, y: 4, z: 8, core: 2. Of those that a mesh axis runs over, the one named last changes fastest.
Arguments:
- points: float32 [1, 32, 2, 1024], P(None, 'pcol'), may hold values from 0 to 1
- range_length: float32 [1], replicated, may hold values from 0.05 to 0.15
- smoothness: int32 [1], replicated, may hold values from 0 to 2
- sketch_bank: bfloat16 [32, 48, 1024], P('pcol'), may hold values from -6 to 6
- sketch_ids: int32 [4, 8, 1, 32], P(None, 'prow', None, 'pcol'), may hold values from 0 to 31
- tile_ranks: int32 [4, 8, 1, 32], P(None, 'prow', None, 'pcol'), may hold values from 16 to 48
Outputs:
- y_factors: float32 [4, 8, 1, 32, 48, 1024], P(None, 'prow', None, 'pcol')
- c_factors: float32 [4, 8, 1, 32, 48, 1024], P(None, 'prow', None, 'pcol')
- tile_error: float32 [4, 8, 1, 32], P(None, 'prow', None, 'pcol')
- rank_total: int32 [1], replicated
All inputs are finite; a program needn't handle non-finite values.
Results may differ from a plain program's by a relative error of at most 0.0098.
The roundings to bfloat16 on the way count: a program that leaves them out, or rounds other values in their place, can miss the bound.
Values may be sent and summed in bfloat16 or wider, within the bound.
A program may use at most 64 MiB of HBM per device.

v0:
```python
import jax
import jax.numpy as jnp
from jax import lax
from jax.sharding import Mesh
from jax.sharding import PartitionSpec as P

PCOL = ("pcol_0", "pcol_1", "pcol_2")
PROW_PCOL = ("prow", "pcol_0", "pcol_1", "pcol_2")


def joined_along(parts, dim):
    shape = list(parts.shape[1:])
    shape[dim] *= parts.shape[0]
    return jnp.moveaxis(parts, 0, dim).reshape(shape)


def sent_to_all(x, axis):
    copies = jnp.broadcast_to(x, (lax.axis_size(axis), *x.shape))
    return lax.all_to_all(copies, axis, split_axis=0, concat_axis=0, tiled=True)


def collect(x, axis, dim):
    return joined_along(sent_to_all(x, axis), dim)


def one_axis_at_a_time(x, axes):
    for axis in axes:
        x = lax.psum(x, axis)
    return x


def kernel_factors(smoothness, range_length):
    morton_value = smoothness[0].astype(jnp.float32)
    kernel_scale = jnp.sqrt(2.0 * morton_value + 1.0) / range_length[0]
    linear_factor = jnp.where(smoothness[0] >= 1, 1.0, 0.0).astype(jnp.float32)
    squared_distance = jnp.where(smoothness[0] >= 2, 1.0 / 3.0, 0.0).astype(jnp.float32)
    return (kernel_scale, linear_factor, squared_distance)


def covariance_tile(row_locations, column_locations, kernel_scale, linear_factor, squared_distance):
    offset_horizontal = row_locations[0][:, None] - column_locations[0][None, :]
    offset_vertical = row_locations[1][:, None] - column_locations[1][None, :]
    scaled_distance = kernel_scale * jnp.sqrt(
        offset_horizontal * offset_horizontal + offset_vertical * offset_vertical
    )
    return (
        1.0 + linear_factor * scaled_distance + squared_distance * scaled_distance * scaled_distance
    ) * jnp.exp(-scaled_distance)


def compress(tile_low, sketch, rank):
    keep = jnp.arange(sketch.shape[0]) < rank
    sketch = jnp.where(keep[:, None], sketch, jnp.zeros_like(sketch))
    sketched = lax.dot_general(
        sketch, tile_low, (((1,), (1,)), ((), ())), preferred_element_type=jnp.float32
    )
    product = jnp.dot(sketched.astype(jnp.bfloat16), tile_low, preferred_element_type=jnp.float32)
    gram = jnp.dot(sketched, sketched.T, precision=lax.Precision.HIGHEST)
    shift = 0.1 * jnp.trace(gram) / rank.astype(jnp.float32)
    gram = gram + jnp.diag(jnp.where(keep, shift, jnp.ones_like(shift)))
    factor = jnp.linalg.cholesky(gram)
    coeffs = jax.scipy.linalg.cho_solve((factor, True), product)
    approx = lax.dot_general(
        sketched, coeffs, (((0,), (0,)), ((), ())), precision=lax.Precision.HIGHEST
    )
    error = tile_low.astype(jnp.float32) - approx
    return (sketched, coeffs, jnp.sum(error * error))


def per_device(points, range_length, smoothness, sketch_bank, sketch_ids, tile_ranks):
    row_count = lax.axis_size("prow")
    col_count = lax.axis_size(PCOL)
    row_place = lax.axis_index("prow")
    col_place = lax.axis_index(PCOL)
    row_tiles = sketch_ids.shape[0]
    col_tiles = sketch_ids.shape[2]
    tile_size = points.shape[3]
    sketch_rows = sketch_bank.shape[1]
    slots_total = row_tiles * col_tiles
    tiles_across = col_tiles * col_count
    kernel_scale, linear_factor, squared_distance = kernel_factors(smoothness, range_length)
    gathered = collect(points, PCOL, 1)
    every_block = gathered.reshape(tiles_across, 2, tile_size)
    row_index = jnp.arange(row_tiles, dtype=jnp.int32) * row_count + row_place
    col_index = jnp.arange(col_tiles, dtype=jnp.int32) * col_count + col_place
    slot_row = jnp.repeat(row_index, col_tiles)
    slot_col = jnp.tile(col_index, row_tiles)
    own_ids = sketch_ids.reshape(slots_total)
    own_ranks = tile_ranks.reshape(slots_total)
    lower = slot_col <= slot_row
    offdiag = slot_col < slot_row
    ranks_local = jnp.sum(jnp.where(offdiag, own_ranks, 0))
    rank_sum = one_axis_at_a_time(ranks_local, PROW_PCOL)
    bank_whole = lax.all_gather(sketch_bank, PCOL, axis=0, tiled=True)
    chosen = bank_whole[own_ids]
    row_points_all = every_block[slot_row]
    col_points_all = every_block[slot_col]

    def one_tile(row_locations, column_locations, sketch, rank):
        tile_block = covariance_tile(
            row_locations, column_locations, kernel_scale, linear_factor, squared_distance
        )
        norm_sq = jnp.sum(tile_block * tile_block)
        sketched, coeffs, err_sq = compress(tile_block.astype(jnp.bfloat16), sketch, rank)
        return (sketched, coeffs, norm_sq, err_sq)

    def mapped(inputs):
        return one_tile(inputs[0], inputs[1], inputs[2], inputs[3])

    sketched_all, coeffs_all, norm_all, err_all = lax.map(
        mapped, (row_points_all, col_points_all, chosen, own_ranks)
    )
    norm_local = jnp.sum(jnp.where(lower, jnp.where(offdiag, 2.0, 1.0) * norm_all, 0.0))
    total = one_axis_at_a_time(norm_local, PROW_PCOL)
    errors = (
        jnp.where(offdiag, jnp.sqrt(err_all), jnp.sqrt(norm_all)) * tiles_across / jnp.sqrt(total)
    )
    errors = jnp.where(lower, errors, 0.0)
    out_shape = (row_tiles, 1, col_tiles, 1, sketch_rows, tile_size)
    y_out = jnp.where(offdiag[:, None, None], sketched_all, 0.0).reshape(out_shape)
    c_out = jnp.where(offdiag[:, None, None], coeffs_all, 0.0).reshape(out_shape)
    err_out = errors.reshape(row_tiles, 1, col_tiles, 1)
    rank_out = rank_sum.reshape(1)
    return (y_out, c_out, err_out, rank_out)


def solution(mesh):
    split = Mesh(
        mesh.devices.reshape(mesh.shape["prow"], 4, 4, 2), ("prow", "pcol_0", "pcol_1", "pcol_2")
    )
    placed = (
        P(None, PCOL, None, None),
        P(),
        P(),
        P(PCOL, None, None),
        P(None, "prow", None, PCOL),
        P(None, "prow", None, PCOL),
    )
    return jax.shard_map(
        per_device,
        mesh=split,
        in_specs=placed,
        out_specs=(
            P(None, "prow", None, PCOL, None, None),
            P(None, "prow", None, PCOL, None, None),
            P(None, "prow", None, PCOL),
            P(),
        ),
        check_vma=False,
    )
```

profile of v0, /device:TPU:1, one launch (start us, length us, event | category | flops | bytes accessed | tf_op | source)
XLA Modules:
  0.0 285.3 jit_solution(14311572031564186619)
XLA Ops:
  7.2 0.7 all-gather.2.cloned.1.call-update
  7.9 1.5 broadcast_in_dim.93
  9.4 8.6 %all-to-all-start = ((f32[32,1,1,2,1024]{4,3,2,1,0:T(2,128)}), f32[32,1,1,2,1024]{4,3,2,1,0:T(2,128)S(1)}, u32[]{:S(2)}, u32[]{:S(2)}) async-start(f32[32,1,1,2,1024]{4,3,2,1,0:T(2,128)} %broadcast_in_dim.93), calls=%async_computation | async-start | bytes 524288 | tf_op jit(solution)/shard_map/all_to_all | solution.py:19
  18.0 0.7 fusion.23
  20.1 1.3 select_reduce_fusion.2
  21.4 5.4 %all-to-all-done = f32[32,1,1,2,1024]{4,3,2,1,0:T(2,128)S(1)} async-done(((f32[32,1,1,2,1024]{4,3,2,1,0:T(2,128)}), f32[32,1,1,2,1024]{4,3,2,1,0:T(2,128)S(1)}, u32[]{:S(2)}, u32[]{:S(2)}) %all-to-all-start) | async-done | bytes 262176 | tf_op jit(solution)/shard_map/all_to_all | solution.py:19
  28.0 36.6 %all-gather.2.cloned.1.call-done = bf16[32,48,1024]{2,1,0:T(8,128)(2,1)} async-done(((bf16[1,48,1024]{2,1,0:T(8,128)(2,1)}), bf16[32,48,1024]{2,1,0:T(8,128)(2,1)}) %all-gather.2.cloned.1.call-update) | async-done | bytes 3145744 | tf_op jit(solution)/shard_map/all_gather | solution.py:94
  64.6 2.5 gather_fusion
  67.2 136.1 %while.17 = (s32[]{:T(128)}, f32[4,48,1024]{2,1,0:T(8,128)S(1)}, f32[4,48,1024]{2,1,0:T(8,128)S(1)}, f32[4]{0:T(128)S(1)}, f32[4]{0:T(128)S(1)}, /*index=5*/s32[...) while((s32[]{:T(128)}, f32[4,48,1024]{2,1,0:T(8,128)S(1)}, ...), condition=%wide.region_6.7_spmd.clone, body=%wide.region_0.6_spmd.sunk.clone | while | flops 954344128 | bytes 2675283 | solution.py:110
  68.5 0.7 iota_compare_fusion.6
  69.2 4.2 %multiply_reduce_fusion.6 = f32[]{:T(128)} fusion(f32[]{:T(128)} %get-tuple-element.278, f32[1024]{0:T(1024)S(1)} %bitcast.123, f32[1024]{0:T(1024)S(1)} %bitcast.127, f32[1024]{0:T(1024)S(1)} %bitcast.119, f32[1024]{0:T(1024)S(1)} %bitcast.131, f32[]{:T(128)} %get-tuple-element.275, f32[]{:T(128)} %get-tuple-element.274), kind=kLoop, calls=%fused_computation.7.clone.1.clone | loop fusion | flops 15728639 | bytes 16400 | tf_op jit(solution)/shard_map/while/body/eval_jaxpr/reduce_sum | solution.py:103
  73.4 0.8 dynamic_update_slice.26
  74.2 3.1 %bitcast_dynamic-update-slice_fusion.6 = (f32[4,48,1024]{2,1,0:T(8,128)S(1)}, f32[48,1024]{1,0:T(8,128)S(1)}) fusion(f32[4,48,1024]{2,1,0:T(8,128)S(1)} %get-tuple-element.256, s32[]{:T(128)S(6)} %copy.24, f32[]{:T(128)} %get-tuple-element.278, f32[1024]{0:T(1024)S(1)} %bitcast.124, f32[1024]{0:T(1024)S(1)} %bitcast.128, ...), kind=kOutput, calls=%fused_computation.12.clone.1.clone | convolution fusion | flops 115392512 | bytes 509452 | tf_op jit(solution)/shard_map/while/body/eval_jaxpr/dot_general | solution.py:54
  77.4 1.0 select_reduce_fusion.7
  79.1 0.7 broadcast_select_fusion.3
  79.9 4.4 %cholesky.73 = f32[48,48]{1,0:T(8,128)S(1)} custom-call(f32[48,48]{1,0:T(8,128)S(1)} %fusion.68), custom_call_target="Cholesky" | custom-call | tf_op jit(solution)/shard_map/while/body/eval_jaxpr/jit(cholesky)/cholesky | solution.py:61
  85.0 0.7 fusion.69
  85.6 3.7 %custom-call.20 = f32[1,48,48]{1,2,0:T(8,128)S(1)} custom-call(f32[1,48,48]{2,1,0:T(8,128)S(1)} %fusion.69), custom_call_target="InvertDiagBlocksLowerTriangular" | custom-call | tf_op jit(solution)/shard_map/while/body/eval_jaxpr/jit(_cho_solve)/triangular_solve | solution.py:62
  89.3 3.2 %fusion.67 = f32[48,1024]{1,0:T(8,128)S(1)} fusion(f32[]{:T(128)} %get-tuple-element.278, f32[1024]{0:T(1024)S(1)} %bitcast.125, f32[1024]{0:T(1024)S(1)} %bitcast.129, f32[1024]{0:T(1024)S(1)} %bitcast.121, f32[1024]{0:T(1024)S(1)} %bitcast.133, f32[]{:T(128)} %get-tuple-element.275, f32[]{:T(128)} %get-tuple-element.274, ...), kind=kOutput, calls=%fused_computation.9.clone.1.clone | convolution fusion | flops 115392512 | bytes 409612 | tf_op jit(solution)/shard_map/while/body/eval_jaxpr/dot_general | solution.py:57
  93.1 7.4 %multiply_reduce_fusion.7 = f32[]{:T(128)} fusion(f32[48,1024]{1,0:T(8,128)S(1)} %get-tuple-element.222, f32[48,1024]{1,0:T(8,128)S(1)} %get-tuple-element.226, f32[]{:T(128)} %get-tuple-element.278, f32[1024]{0:T(1024)S(1)} %bitcast.126, f32[1024]{0:T(1024)S(1)} %bitcast.130, f32[1024]{0:T(1024)S(1)} %bitcast.122, f32[1024]{0:T(1024)S(1)} %bitcast.134, ...), kind=kOutput, calls=%fused_computation.6.clone.1.clone | convolution fusion | flops 622854144 | bytes 409616 | tf_op jit(solution)/shard_map/while/body/eval_jaxpr/dot_general | solution.py:63
  100.5 0.8 dynamic_update_slice.27
  102.5 0.7 iota_compare_fusion.6
  103.2 4.2 %multiply_reduce_fusion.6 = f32[]{:T(128)} fusion(f32[]{:T(128)} %get-tuple-element.278, f32[1024]{0:T(1024)S(1)} %bitcast.123, f32[1024]{0:T(1024)S(1)} %bitcast.127, f32[1024]{0:T(1024)S(1)} %bitcast.119, f32[1024]{0:T(1024)S(1)} %bitcast.131, f32[]{:T(128)} %get-tuple-element.275, f32[]{:T(128)} %get-tuple-element.274), kind=kLoop, calls=%fused_computation.7.clone.1.clone | loop fusion | flops 15728639 | bytes 16400 | tf_op jit(solution)/shard_map/while/body/eval_jaxpr/reduce_sum | solution.py:103
  107.4 0.8 dynamic_update_slice.26
  108.2 3.1 %bitcast_dynamic-update-slice_fusion.6 = (f32[4,48,1024]{2,1,0:T(8,128)S(1)}, f32[48,1024]{1,0:T(8,128)S(1)}) fusion(f32[4,48,1024]{2,1,0:T(8,128)S(1)} %get-tuple-element.256, s32[]{:T(128)S(6)} %copy.24, f32[]{:T(128)} %get-tuple-element.278, f32[1024]{0:T(1024)S(1)} %bitcast.124, f32[1024]{0:T(1024)S(1)} %bitcast.128, ...), kind=kOutput, calls=%fused_computation.12.clone.1.clone | convolution fusion | flops 115392512 | bytes 509452 | tf_op jit(solution)/shard_map/while/body/eval_jaxpr/dot_general | solution.py:54
  111.4 1.0 select_reduce_fusion.7
  113.1 0.7 broadcast_select_fusion.3
  113.9 4.4 %cholesky.73 = f32[48,48]{1,0:T(8,128)S(1)} custom-call(f32[48,48]{1,0:T(8,128)S(1)} %fusion.68), custom_call_target="Cholesky" | custom-call | tf_op jit(solution)/shard_map/while/body/eval_jaxpr/jit(cholesky)/cholesky | solution.py:61
  119.0 0.7 fusion.69
  119.6 3.7 %custom-call.20 = f32[1,48,48]{1,2,0:T(8,128)S(1)} custom-call(f32[1,48,48]{2,1,0:T(8,128)S(1)} %fusion.69), custom_call_target="InvertDiagBlocksLowerTriangular" | custom-call | tf_op jit(solution)/shard_map/while/body/eval_jaxpr/jit(_cho_solve)/triangular_solve | solution.py:62
  123.3 3.2 %fusion.67 = f32[48,1024]{1,0:T(8,128)S(1)} fusion(f32[]{:T(128)} %get-tuple-element.278, f32[1024]{0:T(1024)S(1)} %bitcast.125, f32[1024]{0:T(1024)S(1)} %bitcast.129, f32[1024]{0:T(1024)S(1)} %bitcast.121, f32[1024]{0:T(1024)S(1)} %bitcast.133, f32[]{:T(128)} %get-tuple-element.275, f32[]{:T(128)} %get-tuple-element.274, ...), kind=kOutput, calls=%fused_computation.9.clone.1.clone | convolution fusion | flops 115392512 | bytes 409612 | tf_op jit(solution)/shard_map/while/body/eval_jaxpr/dot_general | solution.py:57
  127.2 7.4 %multiply_reduce_fusion.7 = f32[]{:T(128)} fusion(f32[48,1024]{1,0:T(8,128)S(1)} %get-tuple-element.222, f32[48,1024]{1,0:T(8,128)S(1)} %get-tuple-element.226, f32[]{:T(128)} %get-tuple-element.278, f32[1024]{0:T(1024)S(1)} %bitcast.126, f32[1024]{0:T(1024)S(1)} %bitcast.130, f32[1024]{0:T(1024)S(1)} %bitcast.122, f32[1024]{0:T(1024)S(1)} %bitcast.134, ...), kind=kOutput, calls=%fused_computation.6.clone.1.clone | convolution fusion | flops 622854144 | bytes 409616 | tf_op jit(solution)/shard_map/while/body/eval_jaxpr/dot_general | solution.py:63
  134.5 0.8 dynamic_update_slice.27
  136.5 0.7 iota_compare_fusion.6
  137.2 4.2 %multiply_reduce_fusion.6 = f32[]{:T(128)} fusion(f32[]{:T(128)} %get-tuple-element.278, f32[1024]{0:T(1024)S(1)} %bitcast.123, f32[1024]{0:T(1024)S(1)} %bitcast.127, f32[1024]{0:T(1024)S(1)} %bitcast.119, f32[1024]{0:T(1024)S(1)} %bitcast.131, f32[]{:T(128)} %get-tuple-element.275, f32[]{:T(128)} %get-tuple-element.274), kind=kLoop, calls=%fused_computation.7.clone.1.clone | loop fusion | flops 15728639 | bytes 16400 | tf_op jit(solution)/shard_map/while/body/eval_jaxpr/reduce_sum | solution.py:103
  141.5 0.8 dynamic_update_slice.26
  142.3 3.1 %bitcast_dynamic-update-slice_fusion.6 = (f32[4,48,1024]{2,1,0:T(8,128)S(1)}, f32[48,1024]{1,0:T(8,128)S(1)}) fusion(f32[4,48,1024]{2,1,0:T(8,128)S(1)} %get-tuple-element.256, s32[]{:T(128)S(6)} %copy.24, f32[]{:T(128)} %get-tuple-element.278, f32[1024]{0:T(1024)S(1)} %bitcast.124, f32[1024]{0:T(1024)S(1)} %bitcast.128, ...), kind=kOutput, calls=%fused_computation.12.clone.1.clone | convolution fusion | flops 115392512 | bytes 509452 | tf_op jit(solution)/shard_map/while/body/eval_jaxpr/dot_general | solution.py:54
  145.4 1.0 select_reduce_fusion.7
  147.1 0.7 broadcast_select_fusion.3
  147.9 4.4 %cholesky.73 = f32[48,48]{1,0:T(8,128)S(1)} custom-call(f32[48,48]{1,0:T(8,128)S(1)} %fusion.68), custom_call_target="Cholesky" | custom-call | tf_op jit(solution)/shard_map/while/body/eval_jaxpr/jit(cholesky)/cholesky | solution.py:61
  153.0 0.7 fusion.69
  153.7 3.7 %custom-call.20 = f32[1,48,48]{1,2,0:T(8,128)S(1)} custom-call(f32[1,48,48]{2,1,0:T(8,128)S(1)} %fusion.69), custom_call_target="InvertDiagBlocksLowerTriangular" | custom-call | tf_op jit(solution)/shard_map/while/body/eval_jaxpr/jit(_cho_solve)/triangular_solve | solution.py:62
  157.3 3.2 %fusion.67 = f32[48,1024]{1,0:T(8,128)S(1)} fusion(f32[]{:T(128)} %get-tuple-element.278, f32[1024]{0:T(1024)S(1)} %bitcast.125, f32[1024]{0:T(1024)S(1)} %bitcast.129, f32[1024]{0:T(1024)S(1)} %bitcast.121, f32[1024]{0:T(1024)S(1)} %bitcast.133, f32[]{:T(128)} %get-tuple-element.275, f32[]{:T(128)} %get-tuple-element.274, ...), kind=kOutput, calls=%fused_computation.9.clone.1.clone | convolution fusion | flops 115392512 | bytes 409612 | tf_op jit(solution)/shard_map/while/body/eval_jaxpr/dot_general | solution.py:57
  161.2 7.4 %multiply_reduce_fusion.7 = f32[]{:T(128)} fusion(f32[48,1024]{1,0:T(8,128)S(1)} %get-tuple-element.222, f32[48,1024]{1,0:T(8,128)S(1)} %get-tuple-element.226, f32[]{:T(128)} %get-tuple-element.278, f32[1024]{0:T(1024)S(1)} %bitcast.126, f32[1024]{0:T(1024)S(1)} %bitcast.130, f32[1024]{0:T(1024)S(1)} %bitcast.122, f32[1024]{0:T(1024)S(1)} %bitcast.134, ...), kind=kOutput, calls=%fused_computation.6.clone.1.clone | convolution fusion | flops 622854144 | bytes 409616 | tf_op jit(solution)/shard_map/while/body/eval_jaxpr/dot_general | solution.py:63
  168.6 0.8 dynamic_update_slice.27
  171.2 4.2 %multiply_reduce_fusion.6 = f32[]{:T(128)} fusion(f32[]{:T(128)} %get-tuple-element.278, f32[1024]{0:T(1024)S(1)} %bitcast.123, f32[1024]{0:T(1024)S(1)} %bitcast.127, f32[1024]{0:T(1024)S(1)} %bitcast.119, f32[1024]{0:T(1024)S(1)} %bitcast.131, f32[]{:T(128)} %get-tuple-element.275, f32[]{:T(128)} %get-tuple-element.274), kind=kLoop, calls=%fused_computation.7.clone.1.clone | loop fusion | flops 15728639 | bytes 16400 | tf_op jit(solution)/shard_map/while/body/eval_jaxpr/reduce_sum | solution.py:103
  175.5 0.8 dynamic_update_slice.26
  176.3 3.1 %bitcast_dynamic-update-slice_fusion.6 = (f32[4,48,1024]{2,1,0:T(8,128)S(1)}, f32[48,1024]{1,0:T(8,128)S(1)}) fusion(f32[4,48,1024]{2,1,0:T(8,128)S(1)} %get-tuple-element.256, s32[]{:T(128)S(6)} %copy.24, f32[]{:T(128)} %get-tuple-element.278, f32[1024]{0:T(1024)S(1)} %bitcast.124, f32[1024]{0:T(1024)S(1)} %bitcast.128, ...), kind=kOutput, calls=%fused_computation.12.clone.1.clone | convolution fusion | flops 115392512 | bytes 509452 | tf_op jit(solution)/shard_map/while/body/eval_jaxpr/dot_general | solution.py:54
  179.4 1.0 select_reduce_fusion.7
  182.0 4.4 %cholesky.73 = f32[48,48]{1,0:T(8,128)S(1)} custom-call(f32[48,48]{1,0:T(8,128)S(1)} %fusion.68), custom_call_target="Cholesky" | custom-call | tf_op jit(solution)/shard_map/while/body/eval_jaxpr/jit(cholesky)/cholesky | solution.py:61
  187.0 0.7 fusion.69
  187.7 3.7 %custom-call.20 = f32[1,48,48]{1,2,0:T(8,128)S(1)} custom-call(f32[1,48,48]{2,1,0:T(8,128)S(1)} %fusion.69), custom_call_target="InvertDiagBlocksLowerTriangular" | custom-call | tf_op jit(solution)/shard_map/while/body/eval_jaxpr/jit(_cho_solve)/triangular_solve | solution.py:62
  191.4 3.2 %fusion.67 = f32[48,1024]{1,0:T(8,128)S(1)} fusion(f32[]{:T(128)} %get-tuple-element.278, f32[1024]{0:T(1024)S(1)} %bitcast.125, f32[1024]{0:T(1024)S(1)} %bitcast.129, f32[1024]{0:T(1024)S(1)} %bitcast.121, f32[1024]{0:T(1024)S(1)} %bitcast.133, f32[]{:T(128)} %get-tuple-element.275, f32[]{:T(128)} %get-tuple-element.274, ...), kind=kOutput, calls=%fused_computation.9.clone.1.clone | convolution fusion | flops 115392512 | bytes 409612 | tf_op jit(solution)/shard_map/while/body/eval_jaxpr/dot_general | solution.py:57
  195.2 7.4 %multiply_reduce_fusion.7 = f32[]{:T(128)} fusion(f32[48,1024]{1,0:T(8,128)S(1)} %get-tuple-element.222, f32[48,1024]{1,0:T(8,128)S(1)} %get-tuple-element.226, f32[]{:T(128)} %get-tuple-element.278, f32[1024]{0:T(1024)S(1)} %bitcast.126, f32[1024]{0:T(1024)S(1)} %bitcast.130, f32[1024]{0:T(1024)S(1)} %bitcast.122, f32[1024]{0:T(1024)S(1)} %bitcast.134, ...), kind=kOutput, calls=%fused_computation.6.clone.1.clone | convolution fusion | flops 622854144 | bytes 409616 | tf_op jit(solution)/shard_map/while/body/eval_jaxpr/dot_general | solution.py:63
  202.6 0.8 dynamic_update_slice.27
  204.0 11.7 %psum.60 = s32[]{:T(128)} all-reduce(s32[]{:T(128)} %select_reduce_fusion.2), channel_id=1, replica_groups=mesh['prow'=8,'pcol_0'=4,'pcol_1'=4,'pcol_2'=2] {'prow'}, use_global_device_ids=true, to_apply=%region_13.14 | all-reduce | flops 1 | bytes 8 | tf_op jit(solution)/shard_map/psum | solution.py:28
  215.6 11.8 %psum.56 = f32[]{:T(128)} all-reduce(f32[]{:T(128)} %fusion.22), channel_id=1, replica_groups=mesh['prow'=8,'pcol_0'=4,'pcol_1'=4,'pcol_2'=2] {'prow'}, use_global_device_ids=true, to_apply=%region_8.9 | all-reduce | flops 1 | bytes 8 | tf_op jit(solution)/shard_map/psum | solution.py:28
  227.4 6.9 %psum.61 = s32[]{:T(128)} all-reduce(s32[]{:T(128)} %psum.60), channel_id=1, replica_groups=mesh['prow'=8,'pcol_0'=4,'pcol_1'=4,'pcol_2'=2] {'pcol_0'}, use_global_device_ids=true, to_apply=%region_14.15 | all-reduce | flops 1 | bytes 8 | tf_op jit(solution)/shard_map/psum | solution.py:28
  234.3 8.1 %psum.57 = f32[]{:T(128)} all-reduce(f32[]{:T(128)} %psum.56), channel_id=1, replica_groups=mesh['prow'=8,'pcol_0'=4,'pcol_1'=4,'pcol_2'=2] {'pcol_0'}, use_global_device_ids=true, to_apply=%region_9.10 | all-reduce | flops 1 | bytes 8 | tf_op jit(solution)/shard_map/psum | solution.py:28
  242.4 6.2 %psum.62 = s32[]{:T(128)} all-reduce(s32[]{:T(128)} %psum.61), channel_id=1, replica_groups=mesh['prow'=8,'pcol_0'=4,'pcol_1'=4,'pcol_2'=2] {'pcol_1'}, use_global_device_ids=true, to_apply=%region_15.16 | all-reduce | flops 1 | bytes 8 | tf_op jit(solution)/shard_map/psum | solution.py:28
  248.6 7.7 %psum.58 = f32[]{:T(128)} all-reduce(f32[]{:T(128)} %psum.57), channel_id=1, replica_groups=mesh['prow'=8,'pcol_0'=4,'pcol_1'=4,'pcol_2'=2] {'pcol_1'}, use_global_device_ids=true, to_apply=%region_10.11 | all-reduce | flops 1 | bytes 8 | tf_op jit(solution)/shard_map/psum | solution.py:28
  256.3 16.5 %psum.63 = s32[1]{0:T(128)} all-reduce(s32[1]{0:T(128)} %bitcast.25), channel_id=1, replica_groups=mesh['prow'=8,'pcol_0'=4,'pcol_1'=4,'pcol_2'=2] {'pcol_2'}, use_global_device_ids=true, to_apply=%region_16.17 | all-reduce | flops 1 | bytes 8 | tf_op jit(solution)/shard_map/psum | solution.py:28
  272.8 3.1 %psum.59 = f32[]{:T(128)} all-reduce(f32[]{:T(128)} %psum.58), channel_id=1, replica_groups=mesh['prow'=8,'pcol_0'=4,'pcol_1'=4,'pcol_2'=2] {'pcol_2'}, use_global_device_ids=true, to_apply=%region_11.12 | all-reduce | flops 1 | bytes 8 | tf_op jit(solution)/shard_map/psum | solution.py:28
  277.1 1.4 select_bitcast_fusion
  (51 shorter events, 12.2 us)
Async XLA Ops:
  7.2 60.0 %copy-start = (s32[4,1,1,1]{0,3,2,1:T(1,128)S(1)}, s32[4,1,1,1]{0,3,2,1:T(1,128)}, u32[]{:S(2)}) copy-start(s32[4,1,1,1]{0,3,2,1:T(1,128)} %param.13) | copy-start | bytes 52
  7.2 57.4 %all-gather.2.cloned.1.call-start = ((), (), s32[]{:S(2)}) async-start(), calls=%async_computation.1 | async-start | bytes 3244032 | tf_op jit(solution)/shard_map/all_gather | solution.py:94
  9.4 17.5 %all-to-all-start = ((f32[32,1,1,2,1024]{4,3,2,1,0:T(2,128)}), f32[32,1,1,2,1024]{4,3,2,1,0:T(2,128)S(1)}, u32[]{:S(2)}, u32[]{:S(2)}) async-start(f32[32,1,1,2,1024]{4,3,2,1,0:T(2,128)} %broadcast_in_dim.93), calls=%async_computation | async-start | bytes 524288 | tf_op jit(solution)/shard_map/all_to_all | solution.py:19
Sparse Core Ops, SparseCore 0:
  10.5 53.9 all-gather.1
where the time goes:
time: 286 us; the launch traced here: 285 us
  blocking collectives  71.9 us (25%)
  other arithmetic  64.6 us (23%)
  matrix products  61.3 us (21%)
  waiting for transfers between devices  42.7 us (15%)
  between operations  16.2 us (6%)
  local copies, waits for them, and re-layouts  14.2 us (5%)
  starting transfers between devices  8.61 us (3%)
  loops' own time  5.85 us (2%)
    psum x8, blocking collectives, one_axis_at_a_time(): x = lax.psum(x, axis)  71.9 us
    all_gather x1, waiting for transfers between devices, per_device(): bank_whole = lax.all_gather(sketch_bank, PCOL, axis=0, tiled=True)  36.6 us
    dot_general x4, matrix products, compress(): lax.dot_general(sketched, coeffs, (((0,), (0,)), ((), ())), precision=lax...  29.4 us
    another operation x12, other arithmetic, compress(): factor = jnp.linalg.cholesky(gram)  20.2 us
    another operation x8, other arithmetic, compress(): coeffs = jax.scipy.linalg.cho_solve((factor, True), product)  17.3 us
    reduce_sum x4, other arithmetic, one_tile(): norm_sq = jnp.sum(tile_block * tile_block)  17 us
    dot_general x4, matrix products, compress(): jnp.dot(sketched.astype(jnp.bfloat16), tile_low, preferred_element_type=j...  12.7 us
    dot_general x4, matrix products, compress(): lax.dot_general(sketch, tile_low, (((1,), (1,)), ((), ())), preferred_ele...  12.6 us
  transfers between devices with their start and end apart: 2, of which 2 were waited for; matrix products, arithmetic and copies ran while one was open for 2% of the time, Pallas kernels for 0%

commit v1 on v0

v1 whole, which is shorter than its diff:
```python
import functools
import math

import jax
import jax.numpy as jnp
from jax import lax
from jax.experimental import pallas as pl
from jax.experimental.pallas import tpu as pltpu
from jax.sharding import PartitionSpec as P

MESH = pl.DeviceIdType.MESH
LOG2E = math.log2(math.e)
F32 = jnp.float32
BF16 = jnp.bfloat16
LANES = 128
ROWS = 32
NT = (((1,), (1,)), ((), ()))
TN = (((0,), (0,)), ((), ()))


def kernel(dims, pts, sketch, reach, smooth, ids, ranks, y_out, c_out, err_out, rank_out,
           rows, bank, low, row_x, row_y, col_x, col_y, prod, inv, norms, sums_z, sums_p, message,
           pts_send, pts_recv, own_sem, first_send, first_recv, second_send, second_recv,
           half_send, half_recv, mirror_send, mirror_recv, z_send, z_recv, p_send, p_recv):
    slots, n_row, n_col, nb, rmax = dims
    p = lax.axis_index("prow")
    q = lax.axis_index("pcol")
    y, x, core = q // 8, lax.rem(q // 2, 4), lax.rem(q, 2)
    partner = q + 1 - 2 * core
    half = nb // 2

    def place(e, f):
        dy = core * e + (1 - core) * f
        dx = (1 - core) * e + core * f
        return lax.rem(y + dy + 8, 4) * 8 + lax.rem(x + dx + 8, 4) * 2 + core

    barrier = pltpu.get_barrier_semaphore()
    for d in range(1, n_col):
        pl.semaphore_signal(barrier, inc=1, device_id={"pcol": lax.rem(q + d, n_col)}, device_id_type=MESH)
    for d in range(1, n_row):
        pl.semaphore_signal(barrier, inc=1, device_id={"prow": lax.rem(p + d, n_row)}, device_id_type=MESH)
    pl.semaphore_wait(barrier, n_col - 1 + n_row - 1)

    is_source = lax.rem(q, n_row) == p
    own_slot = q // n_row

    def point_copy(d):
        return pltpu.make_async_remote_copy(
            pts, rows.at[own_slot], pts_send.at[d], pts_recv.at[own_slot],
            device_id={"pcol": q - d}, device_id_type=MESH)

    for d in range(1, n_col):
        @pl.when(is_source & (q >= d))
        def _():
            point_copy(d).start()

    own_copies = [pltpu.make_async_copy(sketch, bank.at[q], own_sem.at[0])]
    own_copies[0].start()

    def remote(src, dst, send, recv, target):
        return pltpu.make_async_remote_copy(src, dst, send, recv, device_id={"pcol": target}, device_id_type=MESH)

    def first_copy(s):
        return remote(sketch, bank.at[q], first_send.at[s], first_recv.at[s], place(1 - 2 * s, 0))

    def second_copy(e, s):
        block = place(-e, 0)
        src = sketch if e == 0 else bank.at[block]
        return remote(src, bank.at[block], second_send.at[e, s], second_recv.at[e, s], place(0, 1 - 2 * s))

    def half_copy(e, s):
        cols = pl.ds(s * half, half)
        step = 1 - 2 * s
        if e == 4:
            block, target = place(-step, 0), place(step, 0)
        else:
            block, target = place(-e, -step), place(0, step)
        return remote(bank.at[block, :, cols], bank.at[block, :, cols], half_send.at[e, s], half_recv.at[e, s], target)

    def mirror_copy(e, f):
        block = place(-e, -f)
        src = sketch if e == 0 and f == 0 else bank.at[block]
        return remote(src, bank.at[block], mirror_send.at[e, f], mirror_recv.at[e, f], partner)

    def first_recv_wait(s):
        first_copy(s).wait_recv()

    def step0():
        for s in range(2):
            first_copy(s).start()
            second_copy(0, s).start()
        mirror_copy(0, 0).start()

    def step1():
        for s, e in ((0, 1), (1, 3)):
            first_copy(s).wait_recv()
            half_copy(4, s).start()
            for t in range(2):
                second_copy(e, t).start()
            mirror_copy(e, 0).start()

    def step2():
        for s, f in ((0, 1), (1, 3)):
            second_copy(0, s).wait_recv()
            half_copy(0, s).start()
            mirror_copy(0, f).start()
        for s in range(2):
            half_copy(4, s).wait_recv()
        for t in range(2):
            second_copy(2, t).start()
        mirror_copy(2, 0).start()

    def step_second(e):
        for s, f in ((0, 1), (1, 3)):
            second_copy(e, s).wait_recv()
            half_copy(e, s).start()
            mirror_copy(e, f).start()

    def step_tail(e):
        for s in range(2):
            half_copy(e, s).wait_recv()
        mirror_copy(e, 2).start()

    step0()

    s_val = smooth[0]
    root = jnp.where(s_val >= 2, math.sqrt(5.0), jnp.where(s_val >= 1, math.sqrt(3.0), 1.0)).astype(F32)
    scale = (root * LOG2E) / jnp.full((8, LANES), reach[0], F32)
    linear = jnp.where(s_val >= 1, 1.0 / LOG2E, 0.0).astype(F32)
    square = jnp.where(s_val >= 2, 1.0 / (3.0 * LOG2E * LOG2E), 0.0).astype(F32)

    for cb in range(nb // LANES):
        cols = pl.ds(cb * LANES, LANES)
        col_x[:, cols] = jnp.broadcast_to(pts[0:1, cols], (8, LANES)) * scale
        col_y[:, cols] = jnp.broadcast_to(pts[1:2, cols], (8, LANES)) * scale

    norms[...] = jnp.zeros_like(norms)
    for a in range(slots):
        eye = (lax.broadcasted_iota(jnp.int32, (rmax, rmax), 0) == lax.broadcasted_iota(jnp.int32, (rmax, rmax), 1))
        inv[a] = jnp.where(eye, 1.0, 0.0).astype(F32)

    def prepare(a, source):
        for cb in range(nb // LANES):
            cols = pl.ds(cb * LANES, LANES)
            for c, out in ((0, row_x), (1, row_y)):
                line = source[c:c + 1, cols] * scale[0:1, :]
                out[cols, :] = jnp.broadcast_to(line, (LANES, LANES)).T

    def generate(a, part, parts):
        count = nb // ROWS // parts

        def body(g, acc):
            r0 = pl.multiple_of(g * ROWS, ROWS)
            acc = list(acc)
            for rg in range(ROWS // 16):
                r = pl.multiple_of(r0 + rg * 16, 16)
                rx = row_x[pl.ds(r, 16), :]
                ry = row_y[pl.ds(r, 16), :]
                for cb in range(nb // LANES):
                    cols = pl.ds(cb * LANES, LANES)
                    cx, cy = col_x[:, cols], col_y[:, cols]
                    tiles = []
                    for h in range(2):
                        dx = rx[h * 8:h * 8 + 8] - cx
                        dy = ry[h * 8:h * 8 + 8] - cy
                        d2 = jnp.maximum(dx * dx + dy * dy, 1e-30)
                        t = d2 * lax.rsqrt(d2)
                        value = (1.0 + linear * t + square * d2) * jnp.exp2(-t)
                        acc[h] = acc[h] + value * value
                        tiles.append(value)
                    low[a, pl.ds(r, 16), cols] = jnp.concatenate(tiles, 0).astype(BF16)
            return tuple(acc)

        zero = jnp.zeros((8, LANES), F32)
        acc = lax.fori_loop(part * count, (part + 1) * count, body, (zero, zero))
        norms[a] = norms[a] + (acc[0] + acc[1])

    own_points = own_slot
    def tile_part(a, part, parts):
        row = n_row * a + p

        @pl.when(q <= row)
        def _():
            if part == 0:
                @pl.when(q < row)
                def _():
                    remote(pts, rows.at[a], pts_send.at[0], pts_recv.at[a], partner).wait_recv()
                    prepare(a, rows.at[a])

                @pl.when(q == row)
                def _():
                    prepare(a, pts)
            generate(a, part, parts)

    tile_part(3, 0, 2)
    step1()
    tile_part(3, 1, 2)
    step2()
    tile_part(2, 0, 2)
    step_second(1)
    tile_part(2, 1, 2)
    step_second(3)
    tile_part(1, 0, 2)
    step_tail(0)
    step_second(2)
    tile_part(1, 1, 2)
    step_tail(1)
    tile_part(0, 0, 2)
    step_tail(3)
    tile_part(0, 1, 2)
    step_tail(2)

    share = jnp.zeros((8, LANES), F32)
    rank_share = jnp.int32(0)
    for a in range(slots):
        row = n_row * a + p
        weight = jnp.where(q < row, 2.0, jnp.where(q == row, 1.0, 0.0)).astype(F32)
        share = share + weight * norms[a]
        rank_share = rank_share + jnp.where(q < row, ranks[a], 0)
    lane = lax.broadcasted_iota(jnp.int32, (8, LANES), 1)
    sub = lax.broadcasted_iota(jnp.int32, (8, LANES), 0)
    folded = jnp.sum(share, axis=0, keepdims=True)
    sums_z[p] = jnp.where(sub == 0, jnp.broadcast_to(folded, (8, LANES)),
                          jnp.where((sub == 1) & (lane == 0), rank_share.astype(F32), 0.0))

    def z_copy(d):
        return pltpu.make_async_remote_copy(
            sums_z.at[p], sums_z.at[p], z_send.at[d], z_recv.at[d],
            device_id={"prow": lax.rem(p + d, n_row)}, device_id_type=MESH)

    def p_copy(d):
        return pltpu.make_async_remote_copy(
            sums_p.at[q], sums_p.at[q], p_send.at[d], p_recv.at[d],
            device_id={"pcol": lax.rem(q + d, n_col)}, device_id_type=MESH)

    own_copies[0].wait()
    for e in range(4):
        for f in range(4):
            mirror_copy(e, f).wait_recv()

    for d in range(1, n_row):
        z_copy(d).start()

    def products(a):
        row = n_row * a + p

        @pl.when(q < row)
        def _():
            keep = lax.broadcasted_iota(jnp.int32, (rmax, nb), 0) < ranks[a]
            chosen = jnp.where(keep, bank[ids[a]].astype(F32), 0.0).astype(BF16)
            total = jnp.zeros((rmax, nb), F32)
            for mb in range(nb // 256):
                block = low[a, mb * 256:(mb + 1) * 256, :]
                part = lax.dot_general(chosen, block, NT, preferred_element_type=F32)
                y_out[a, :, mb * 256:(mb + 1) * 256] = part
                total = total + jnp.dot(part.astype(BF16), block, preferred_element_type=F32)
            prod[a] = total
            sketched = y_out[a]
            gram = lax.dot_general(sketched, sketched, NT, precision=lax.Precision.HIGHEST, preferred_element_type=F32)
            ri = lax.broadcasted_iota(jnp.int32, (rmax, rmax), 0)
            ci = lax.broadcasted_iota(jnp.int32, (rmax, rmax), 1)
            diag = ri == ci
            trace = jnp.sum(jnp.where(diag, gram, 0.0), keepdims=True)
            shift = 0.1 * trace / jnp.full((1, 1), ranks[a].astype(F32))
            inv[a] = gram + jnp.where(diag, jnp.where(ri < ranks[a], jnp.broadcast_to(shift, (rmax, rmax)), 1.0), 0.0)

    products(3)
    products(2)
    for d in range(1, n_row):
        z_copy(d).wait_recv()
    plane = sums_z[0]
    for d in range(1, n_row):
        plane = plane + sums_z[d]
    sums_p[q] = plane
    products(1)
    products(0)
    for d in range(1, n_col):
        p_copy(d).start()

    ri = lax.broadcasted_iota(jnp.int32, (rmax, rmax), 0)
    ci = lax.broadcasted_iota(jnp.int32, (rmax, rmax), 1)
    mats = [inv[a] for a in range(slots)]
    for k in range(rmax):
        for a in range(slots):
            m = mats[a]
            r = m[k:k + 1, :]
            c = m[:, k:k + 1]
            d = 1.0 / m[k:k + 1, k:k + 1]
            r = jnp.where(ci[0:1] == k, d, r * d)
            m = jnp.where(ci == k, 0.0, m) - c * r
            mats[a] = jnp.where(ri == k, r, m)
    for a in range(slots):
        inv[a] = mats[a]

    def finish(a):
        row = n_row * a + p

        @pl.when(q < row)
        def _():
            coeffs = jnp.dot(inv[a], prod[a], precision=lax.Precision.HIGHEST, preferred_element_type=F32)
            c_out[a] = coeffs
            c_hi = coeffs.astype(BF16)
            c_lo = (coeffs - c_hi.astype(F32)).astype(BF16)
            right = jnp.concatenate([c_hi, c_hi, c_lo], 0)
            acc = jnp.zeros((8, LANES), F32)
            for mb in range(nb // 128):
                part = y_out[a, :, mb * 128:(mb + 1) * 128]
                hi = part.astype(BF16).astype(F32)
                left = jnp.concatenate([hi, part - hi, hi], 0).T.astype(BF16)
                approx = jnp.dot(left, right, preferred_element_type=F32)
                gap = low[a, mb * 128:(mb + 1) * 128, :].astype(F32) - approx
                gap = gap * gap
                for i in range(16):
                    for j in range(nb // LANES):
                        acc = acc + gap[i * 8:i * 8 + 8, j * LANES:(j + 1) * LANES]
            norms[a] = acc

        @pl.when(q >= row)
        def _():
            y_out[a] = jnp.zeros((rmax, nb), F32)
            c_out[a] = jnp.zeros((rmax, nb), F32)

    for a in range(slots):
        finish(a)

    for d in range(1, n_col):
        p_copy(d).wait_recv()
    whole = sums_p[0]
    for d in range(1, n_col):
        whole = whole + sums_p[d]
    total = jnp.sum(whole[0:1, :], keepdims=True)
    ranks_sum = jnp.sum(whole[1:2, :])
    rank_out[0] = ranks_sum.astype(jnp.int32)
    for a in range(slots):
        row = n_row * a + p
        value = jnp.sum(norms[a], keepdims=True)
        value = jnp.sqrt(value) * (n_row * slots) / jnp.sqrt(total)
        value = jnp.where(q <= row, value, 0.0)
        err_out[a] = value[0, 0]

    for d in range(1, n_col):
        @pl.when(is_source & (q >= d))
        def _():
            point_copy(d).wait_send()
        p_copy(d).wait_send()
    for d in range(1, n_row):
        z_copy(d).wait_send()
    for s in range(2):
        first_copy(s).wait_send()
        for e in range(5):
            half_copy(e, s).wait_send()
        for e in range(4):
            second_copy(e, s).wait_send()
    for e in range(4):
        for f in range(4):
            mirror_copy(e, f).wait_send()


def solution(mesh):
    n_row, n_col = mesh.shape["prow"], mesh.shape["pcol"]

    def per_device(points, range_length, smoothness, sketch_bank, sketch_ids, tile_ranks):
        slots = sketch_ids.shape[0]
        nb = points.shape[3]
        rmax = sketch_bank.shape[1]
        dims = (slots, n_row, n_col, nb, rmax)
        vmem = pl.BlockSpec(memory_space=pltpu.VMEM)
        smem = pl.BlockSpec(memory_space=pltpu.SMEM)
        dma = pltpu.SemaphoreType.DMA
        y_out, c_out, err, rank = pl.pallas_call(
            functools.partial(kernel, dims),
            out_shape=(
                jax.ShapeDtypeStruct((slots, rmax, nb), F32),
                jax.ShapeDtypeStruct((slots, rmax, nb), F32),
                jax.ShapeDtypeStruct((slots,), F32),
                jax.ShapeDtypeStruct((1,), jnp.int32),
            ),
            in_specs=[vmem, vmem, smem, smem, smem, smem],
            out_specs=(vmem, vmem, smem, smem),
            scratch_shapes=[
                pltpu.VMEM((slots, 2, nb), F32),
                pltpu.VMEM((n_col, rmax, nb), BF16),
                pltpu.VMEM((slots, nb, nb), BF16),
                pltpu.VMEM((nb, LANES), F32),
                pltpu.VMEM((nb, LANES), F32),
                pltpu.VMEM((8, nb), F32),
                pltpu.VMEM((8, nb), F32),
                pltpu.VMEM((slots, rmax, nb), F32),
                pltpu.VMEM((slots, rmax, rmax), F32),
                pltpu.VMEM((slots, 8, LANES), F32),
                pltpu.VMEM((n_row, 8, LANES), F32),
                pltpu.VMEM((n_col, 8, LANES), F32),
                pltpu.VMEM((8, LANES), F32),
                dma((n_col,)), dma((slots,)), dma((1,)),
                dma((2,)), dma((2,)), dma((4, 2)), dma((4, 2)),
                dma((5, 2)), dma((5, 2)), dma((4, 4)), dma((4, 4)),
                dma((n_row,)), dma((n_row,)), dma((n_col,)), dma((n_col,)),
            ],
            compiler_params=pltpu.CompilerParams(
                collective_id=0, has_side_effects=True, vmem_limit_bytes=60 * 1024 * 1024),
        )(
            points.reshape(2, nb), sketch_bank.reshape(rmax, nb), range_length, smoothness,
            sketch_ids.reshape(slots), tile_ranks.reshape(slots),
        )
        return (
            y_out.reshape(slots, 1, 1, 1, rmax, nb),
            c_out.reshape(slots, 1, 1, 1, rmax, nb),
            err.reshape(slots, 1, 1, 1),
            rank,
        )

    return jax.shard_map(
        per_device,
        mesh=mesh,
        in_specs=(
            P(None, "pcol", None, None),
            P(),
            P(),
            P("pcol", None, None),
            P(None, "prow", None, "pcol"),
            P(None, "prow", None, "pcol"),
        ),
        out_specs=(
            P(None, "prow", None, "pcol", None, None),
            P(None, "prow", None, "pcol", None, None),
            P(None, "prow", None, "pcol"),
            P(),
        ),
        check_vma=False,
    )
```

time: 286 us -> 61.4 us (0.21)
  the two profiles are of different devices: /device:TPU:1 before, /device:TPU:65 now
where the time goes in v1:
time: 61.4 us; the launch traced here: 61.3 us
  Pallas kernels  54.1 us (88%)
  between operations  3.62 us (6%)
  local copies, waits for them, and re-layouts  3.56 us (6%)
    pallas_call x1, Pallas kernels, per_device(): pl.pallas_call(functools.partial(kernel, dims), out_shape=(jax.ShapeDtype...  54.1 us
    unnamed x7, local copies, waits for them, and re-layouts  3.56 us

profile of v1, /device:TPU:65, one launch (start us, length us, event | category | flops | bytes accessed | tf_op | source)
XLA Modules:
  0.0 61.3 jit_solution(11864608682400598078)
XLA Ops:
  1.9 54.1 %shard_map.93 = (f32[4,48,1024]{2,1,0:T(8,128)}, f32[4,48,1024]{2,1,0:T(8,128)}, f32[4]{0:T(128)}, s32[1]{0:T(128)}) custom-call(f32[2,1024]{1,0:T(2,128)} %bitcast.14, bf16[48,1024]{1,0:T(8,128)(2,1)} %bitcast.13, f32[1]{0:T(128)S(6)} %copy.16.reach, s32[1]{0:T(128)S(6)} %copy.17.smooth, s32[4]{0:T(128)} %bitcast.15, s32[4]{0:T(128)} %bitcast.16), custom_call_target="tpu_custom_call" | custom-call | tf_op jit(solution)/shard_map/pallas_call | solution.py:370
  56.0 0.0 copy-start
  56.0 2.2 %copy.18 = f32[4,1,1,1,48,1024]{5,4,3,2,1,0:T(8,128)} copy(f32[4,1,1,1,48,1024]{5,4,3,2,1,0:T(8,128)} %bitcast.12) | data formatting | bytes 1572864
  58.2 0.0 copy-done
  58.2 0.0 copy-start.1
  58.2 0.9 %copy.19 = f32[4,1,1,1,48,1024]{5,4,3,2,1,0:T(8,128)} copy(f32[4,1,1,1,48,1024]{5,4,3,2,1,0:T(8,128)S(1)} %bitcast.11) | data formatting | bytes 1572864
  59.1 0.0 copy-done.1
  59.1 0.5 copy.20
Async XLA Ops:
  56.0 2.2 %copy-start = (f32[4,48,1024]{2,1,0:T(8,128)S(1)}, f32[4,48,1024]{2,1,0:T(8,128)}, u32[]{:S(2)}) copy-start(f32[4,48,1024]{2,1,0:T(8,128)} %get-tuple-element.9) | copy-start | bytes 2359300
  58.2 0.9 %copy-start.1 = (f32[4]{0:T(128)S(1)}, f32[4]{0:T(128)}, u32[]{:S(2)}) copy-start(f32[4]{0:T(128)} %get-tuple-element.10) | copy-start | bytes 52

commit v2 on v0

v2 whole, which is shorter than its diff:
```python
import functools
import math

import jax
import jax.numpy as jnp
from jax import lax
from jax.experimental import pallas as pl
from jax.experimental.pallas import tpu as pltpu
from jax.sharding import PartitionSpec as P

MESH = pl.DeviceIdType.MESH
LOG2E = math.log2(math.e)
F32 = jnp.float32
BF16 = jnp.bfloat16
LANES = 128
ROWS = 128
VMEM_BYTES = 40 * 1024 * 1024
NT = (((1,), (1,)), ((), ()))


def kernel(dims, pts_in, sketch_in, reach_in, smooth_in, ids_in, ranks_in, y_out, c_out, err_out, rank_out,
           reach, smooth, ids, ranks, pts, rows, far_cols, bank, low, row_x, row_y, col_x, col_y, left, wide, prod, coef, gram_buf, tall, norms, errs,
           zeros, note, far_note, sent_y, sent_c, far_y, far_c, far_err, sums_z, sums_p,
           load_sem, group_send, pts_send, pts_recv, help_send, help_recv, bank_send, bank_recv1, bank_recv2, mirror_recv,
           sum_send, sum_recv, out_sem, zero_sem):
    slots, n_row, n_col, nb, rmax = dims
    p = lax.axis_index("prow")
    q = lax.axis_index("pcol")
    y, x, core = q // 8, lax.rem(q // 2, 4), lax.rem(q, 2)
    partner = q + 1 - 2 * core
    is_home, is_helper = y == 0, y == slots - 1
    pair = lax.rem(q + (slots - 1) * n_row, n_col)
    job_slot = (jnp.where(is_home, 1, slots - 1), 2, y)
    job_on = (q >= 0, y <= 1, q <= n_row * y + p)
    job_off = (q >= 0, y <= 1, q < n_row * y + p)

    def remote(src, dst, send, recv, target):
        return pltpu.make_async_remote_copy(src, dst, send, recv, device_id={"pcol": target}, device_id_type=MESH)

    def all_of(ref, sem):
        pltpu.make_async_copy(ref, ref, sem).wait()

    def place(e, f):
        dy = core * e + (1 - core) * f
        dx = (1 - core) * e + core * f
        return lax.rem(y + dy + 8, 4) * 8 + lax.rem(x + dx + 8, 4) * 2 + core

    loads = [pltpu.make_async_copy(src, dst, load_sem.at[i]) for i, (src, dst) in enumerate((
        (reach_in, reach), (smooth_in, smooth), (ids_in, ids), (ranks_in, ranks), (pts_in, pts),
        (sketch_in, bank.at[q])))]
    barrier = pltpu.get_barrier_semaphore()

    def phase_enter():
        for load in loads:
            load.start()
        for d in range(1, n_col):
            pl.semaphore_signal(barrier, inc=1, device_id={"pcol": lax.rem(q + d, n_col)}, device_id_type=MESH)
        for d in range(1, n_row):
            pl.semaphore_signal(barrier, inc=1, device_id={"prow": lax.rem(p + d, n_row)}, device_id_type=MESH)

    lane = lax.broadcasted_iota(jnp.int32, (8, LANES), 1)
    sub = lax.broadcasted_iota(jnp.int32, (8, LANES), 0)

    zero_copies = [[pltpu.make_async_copy(zeros, out.at[a], zero_sem.at[a]) for a in range(slots)]
                   for out in (y_out, c_out)]

    def phase_setup():
        for load in loads:
            load.wait()
        note[...] = jnp.where(lane == 0, ids[slots - 1], ranks[slots - 1])
        zeros[...] = jnp.zeros((rmax, nb), F32)
        norms[...] = jnp.zeros_like(norms)
        errs[...] = jnp.zeros_like(errs)
        for k in range(3):
            gram_buf[k] = jnp.where(eye, 1.0, 0.0).astype(F32)
        for a in range(slots):
            @pl.when(q >= n_row * a + p)
            def _():
                for i in range(2):
                    zero_copies[i][a].start()

    mat_r = lax.broadcasted_iota(jnp.int32, (rmax, rmax), 0)
    mat_c = lax.broadcasted_iota(jnp.int32, (rmax, rmax), 1)
    eye = mat_r == mat_c

    def phase_barrier():
        pl.semaphore_wait(barrier, n_col - 1 + n_row - 1)

    is_source = lax.rem(q, n_row) == p

    def group_copy(g, i):
        return remote(pts, rows.at[y], group_send.at[g], pts_recv.at[y], g * 8 + i)

    def sends_group(g):
        return is_source & jnp.where(y == slots - 1, (g > 0) & (g < slots - 1), g < y)

    def point_copy(d):
        return remote(pts, rows.at[y], pts_send.at[d], pts_recv.at[y], y * 8 + lax.rem(q + d, 8))

    def sends_points(d):
        return is_source & ((y == slots - 1) | (lax.rem(q, 8) + d >= 8))

    help_copies = (
        lambda: remote(pts, far_cols, help_send.at[0], help_recv.at[0], pair),
        lambda: remote(note, far_note, help_send.at[1], help_recv.at[1], pair),
    )
    back = lax.rem(q + n_row, n_col)
    back_copies = (
        lambda: remote(sent_y, far_y, help_send.at[2], help_recv.at[2], back),
        lambda: remote(sent_c, far_c, help_send.at[3], help_recv.at[3], back),
        lambda: remote(errs.at[0], far_err, help_send.at[4], help_recv.at[4], back),
    )

    def phase_points():
        for g in range(slots - 1):
            @pl.when(sends_group(g))
            def _():
                for i in range(8):
                    group_copy(g, i).start()
        for d in range(1, 8):
            @pl.when(sends_points(d))
            def _():
                point_copy(d).start()

        @pl.when(is_home)
        def _():
            for c in help_copies:
                c().start()

    def first_copy(d):
        return remote(bank.at[q], bank.at[q], bank_send.at[0], bank_recv1.at[d], place(d, 0))

    def second_copy(e, d):
        block = place(-e, 0)
        return remote(bank.at[block], bank.at[block], bank_send.at[0], bank_recv2.at[e], place(0, d))

    def mirror_copy(e, f):
        block = place(-e, -f)
        return remote(bank.at[block], bank.at[block], bank_send.at[0], mirror_recv.at[0], partner)

    def step_own():
        for d in (1, 3, 2):
            first_copy(d).start()
        for d in (1, 3, 2):
            second_copy(0, d).start()
        mirror_copy(0, 0).start()

    def step_first(e):
        first_copy(e).wait_recv()
        for d in (1, 3, 2):
            second_copy(e, d).start()
        mirror_copy(e, 0).start()

    def step_second(e):
        all_of(bank.at[0:3], bank_recv2.at[e])
        for d in (1, 3, 2):
            mirror_copy(e, d).start()

    def prepare_rows(source):
        for cb in range(nb // LANES):
            cols = pl.ds(cb * LANES, LANES)
            for c, out in ((0, row_x), (1, row_y)):
                line = source[c:c + 1, cols] * scale[0:1, :]
                out[cols, :] = jnp.broadcast_to(line, (LANES, LANES)).T

    def prepare_cols(source):
        for cb in range(nb // LANES):
            cols = pl.ds(cb * LANES, LANES)
            col_x[:, cols] = jnp.broadcast_to(source[0:1, cols], (8, LANES)) * scale
            col_y[:, cols] = jnp.broadcast_to(source[1:2, cols], (8, LANES)) * scale

    def generate(k, part, parts):
        count = nb // ROWS // parts

        def body(g, acc):
            r0 = pl.multiple_of(g * ROWS, ROWS)
            acc = list(acc)
            for rg in range(ROWS // 16):
                r = pl.multiple_of(r0 + rg * 16, 16)
                rx = row_x[pl.ds(r, 16), :]
                ry = row_y[pl.ds(r, 16), :]
                for cb in range(nb // LANES):
                    cols = pl.ds(cb * LANES, LANES)
                    cx, cy = col_x[:, cols], col_y[:, cols]
                    tiles = []
                    for h in range(2):
                        dx = rx[h * 8:h * 8 + 8] - cx
                        dy = ry[h * 8:h * 8 + 8] - cy
                        d2 = jnp.maximum(dx * dx + dy * dy, 1e-30)
                        t = d2 * lax.rsqrt(d2)
                        value = (1.0 + linear * t + square * d2) * jnp.exp2(-t)
                        acc[h] = acc[h] + value * value
                        tiles.append(value)
                    low[k, pl.ds(r, 16), cols] = jnp.concatenate(tiles, 0).astype(BF16)
            return tuple(acc)

        zero = jnp.zeros((8, LANES), F32)
        acc = lax.fori_loop(part * count, (part + 1) * count, body, (zero, zero))
        norms[k] = norms[k] + (acc[0] + acc[1])

    def row_block(a):
        @pl.when(q == n_row * a + p)
        def _():
            prepare_rows(pts)

        @pl.when(q != n_row * a + p)
        def _():
            remote(pts, rows.at[a], pts_send.at[0], pts_recv.at[a], partner).wait_recv()
            prepare_rows(rows.at[a])

    def tile_part(k, part):
        @pl.when(job_on[k])
        def _():
            if part == 0 and k == 0:
                @pl.when(is_helper)
                def _():
                    help_copies[0]().wait_recv()
                    help_copies[1]().wait_recv()
                    prepare_cols(far_cols)

                @pl.when(jnp.logical_not(is_helper))
                def _():
                    prepare_cols(pts)
                for a in (1, slots - 1):
                    @pl.when(job_slot[0] == a)
                    def _():
                        row_block(a)
            if part == 0 and k == 1:
                row_block(2)
            if part == 0 and k == 2:
                @pl.when(is_helper)
                def _():
                    prepare_cols(pts)
                for a in range(slots - 1):
                    @pl.when(y == a)
                    def _():
                        row_block(a)
            generate(k, part, 4)

    def z_copy(d):
        return pltpu.make_async_remote_copy(
            sums_z.at[p], sums_z.at[p], sum_send.at[0], sum_recv.at[0],
            device_id={"prow": lax.rem(p + d, n_row)}, device_id_type=MESH)

    def p_copy(d):
        return remote(sums_p.at[q], sums_p.at[q], sum_send.at[1], sum_recv.at[1], lax.rem(q + d, n_col))

    def phase_share():
        share = jnp.zeros((8, LANES), F32)
        for k in range(3):
            weight = jnp.where(job_off[k], 2.0, jnp.where(job_on[k], 1.0, 0.0)).astype(F32)
            share = share + weight * norms[k]
        rank_share = jnp.int32(0)
        for a in range(slots):
            rank_share = rank_share + jnp.where(q < n_row * a + p, ranks[a], 0)
        folded = jnp.sum(share, axis=0, keepdims=True)
        sums_z[p] = jnp.where(sub == 0, jnp.broadcast_to(folded, (8, LANES)),
                              jnp.where((sub == 1) & (lane == 0), rank_share.astype(F32), 0.0))

    def wait_bank():
        all_of(bank.at[0:16], mirror_recv.at[0])

    def send_z():
        for d in range(1, n_row):
            z_copy(d).start()

    def y_copy(k):
        return pltpu.make_async_copy(wide.at[k], y_out.at[job_slot[k]], out_sem.at[0, k])

    def c_copy(k):
        return pltpu.make_async_copy(coef.at[k], c_out.at[job_slot[k]], out_sem.at[1, k])

    def ranks_of(k):
        own = ranks[job_slot[k]]
        return jnp.where(is_helper, far_note[0:1, 1:2][0, 0], own) if k == 0 else own

    def id_of(k):
        own = ids[job_slot[k]]
        return jnp.where(is_helper, far_note[0:1, 0:1][0, 0], own) if k == 0 else own

    def products(k):
        @pl.when(job_off[k])
        def _():
            rank = ranks_of(k)
            keep = lax.broadcasted_iota(jnp.int32, (rmax, nb), 0) < rank
            chosen = jnp.where(keep, bank[id_of(k)].astype(F32), 0.0).astype(BF16)
            triple = jnp.concatenate([chosen, chosen, chosen], 0)
            middle = lax.broadcasted_iota(jnp.int32, (LANES, 3 * rmax), 1)
            middle = (middle >= rmax) & (middle < 2 * rmax)
            tall[...] = lax.dot_general(low[k], triple, NT, preferred_element_type=F32)
            for mb in range(nb // LANES):
                part = tall[mb * LANES:(mb + 1) * LANES, :]
                high = part.astype(BF16).astype(F32)
                left[k, mb * LANES:(mb + 1) * LANES, :] = jnp.where(middle, part - high, high).astype(BF16)
                wide[k, :, mb * LANES:(mb + 1) * LANES] = part[:, :LANES].T[:rmax]
            sketched = wide[k]
            high = sketched.astype(BF16)
            rest = (sketched - high.astype(F32)).astype(BF16)
            if k == 0:
                sent_y[...] = high
            prod[k] = jnp.dot(high, low[k], preferred_element_type=F32)
            both = lax.dot_general(high, jnp.concatenate([high, rest], 0), NT, preferred_element_type=F32)
            cross = both[:, rmax:]
            gram = both[:, :rmax] + (cross + cross.T)
            trace = jnp.sum(jnp.where(eye, gram, 0.0), keepdims=True)
            shift = 0.1 * trace / jnp.full((1, 1), rank.astype(F32))
            gram_buf[k] = gram + jnp.where(
                eye, jnp.where(mat_r < rank, jnp.broadcast_to(shift, (rmax, rmax)), 1.0), 0.0)

    def send_y(k):
        @pl.when(job_off[k])
        def _():
            if k == 0:
                @pl.when(is_helper)
                def _():
                    back_copies[0]().start()

                @pl.when(jnp.logical_not(is_helper))
                def _():
                    y_copy(k).start()
            else:
                y_copy(k).start()

    def invert(jobs):
        mats = [gram_buf[k] for k in jobs]
        b = 8
        row8 = lax.broadcasted_iota(jnp.int32, (b, rmax), 0)
        col8 = lax.broadcasted_iota(jnp.int32, (b, rmax), 1)
        for k0 in range(0, rmax, b):
            spread = [[[jnp.broadcast_to(m[i:i + b, k0 + j:k0 + j + 1], (b, rmax)) for j in range(b)]
                       for i in range(0, rmax, b)] for m in mats]
            for n in range(len(mats)):
                m = mats[n]
                d = list(spread[n][k0 // b])
                for j in range(b):
                    inverse = 1.0 / d[j][j:j + 1, :]
                    for i in range(b):
                        if i != j:
                            f = d[i][j:j + 1, :] * inverse
                            d[i] = jnp.where(row8 == j, f, d[i] - d[j] * f)
                    d[j] = jnp.where(row8 == j, inverse, -(d[j] * inverse))
                panel = m[k0:k0 + b]
                r = d[0] * panel[0:1]
                for j in range(1, b):
                    r = r + d[j] * panel[j:j + 1]
                for j in range(b):
                    r = jnp.where(col8 == k0 + j, d[j], r)
                inside = (col8 >= k0) & (col8 < k0 + b)
                out = []
                for i in range(0, rmax, b):
                    if i == k0:
                        out.append(r)
                        continue
                    piece = jnp.where(inside, 0.0, m[i:i + b])
                    for j in range(b):
                        piece = piece - spread[n][i // b][j] * r[j:j + 1]
                    out.append(piece)
                mats[n] = jnp.concatenate(out, 0)
        return mats

    def finish(k, inverse):
        coeffs = jnp.dot(inverse, prod[k], precision=lax.Precision.HIGHEST, preferred_element_type=F32)
        coef[k] = coeffs
        c_hi = coeffs.astype(BF16)
        c_lo = (coeffs - c_hi.astype(F32)).astype(BF16)
        if k == 0:
            sent_c[...] = c_hi
        right = jnp.concatenate([c_hi, c_hi, c_lo], 0)
        acc = [jnp.zeros((8, LANES), F32) for _ in range(4)]
        width, height = 256, 512
        for nt in range(nb // width):
            for mt in range(nb // height):
                span, cols = slice(mt * height, (mt + 1) * height), slice(nt * width, (nt + 1) * width)
                approx = jnp.dot(left[k, span, :], right[:, cols], preferred_element_type=F32)
                gap = low[k, span, cols].astype(F32) - approx
                for i in range(height // 8):
                    for j in range(width // LANES):
                        piece = gap[i * 8:i * 8 + 8, j * LANES:(j + 1) * LANES]
                        n = (2 * i + j) % 4
                        acc[n] = acc[n] + piece * piece
        errs[k] = (acc[0] + acc[1]) + (acc[2] + acc[3])

    def phase_early():
        @pl.when(is_helper)
        def _():
            finish(0, invert((0,))[0])
            back_copies[1]().start()

    def phase_invert():
        mats = invert((0, 1, 2))
        for k in range(3):
            gram_buf[k] = mats[k]

    def phase_finish(k):
        @pl.when(job_off[k] & jnp.logical_not(is_helper) if k == 0 else job_off[k])
        def _():
            finish(k, gram_buf[k])
            c_copy(k).start()

    def wait_z():
        all_of(sums_z.at[0:n_row - 1], sum_recv.at[0])
        plane = sums_z[0]
        for d in range(1, n_row):
            plane = plane + sums_z[d]
        sums_p[q] = plane

    def send_p():
        for d in range(1, n_col):
            p_copy(d).start()

        @pl.when(is_helper)
        def _():
            back_copies[2]().start()

    def phase_far_y():
        @pl.when(is_home)
        def _():
            back_copies[0]().wait_recv()
            wide[3] = far_y[...].astype(F32)
            pltpu.make_async_copy(wide.at[3], y_out.at[slots - 1], out_sem.at[0, 3]).start()

    def phase_far():
        @pl.when(is_home)
        def _():
            for c in back_copies[1:]:
                c().wait_recv()
            coef[3] = far_c[...].astype(F32)
            pltpu.make_async_copy(coef.at[3], c_out.at[slots - 1], out_sem.at[1, 3]).start()

    def total_error():
        all_of(sums_p.at[0:n_col - 1], sum_recv.at[1])
        whole = sums_p[0]
        for d in range(1, n_col):
            whole = whole + sums_p[d]
        total = jnp.sum(whole[0:1, :], keepdims=True)
        rank_out[0] = jnp.sum(whole[1:2, :]).astype(jnp.int32)
        factor = (n_row * slots) / jnp.sqrt(total)
        values = []
        for k in range(3):
            source = jnp.where(job_off[k], errs[k], norms[k])
            value = jnp.sqrt(jnp.sum(source, keepdims=True)) * factor
            values.append(jnp.where(job_on[k], value, 0.0))
        far = jnp.sqrt(jnp.sum(far_err[...], keepdims=True)) * factor
        for a in range(slots):
            out = jnp.zeros((1, 1), F32)
            for k in range(3):
                mine = (job_slot[k] == a) & job_on[k]
                if k == 0:
                    mine = mine & jnp.logical_not(is_helper)
                out = jnp.where(mine, values[k], out)
            if a == slots - 1:
                out = jnp.where(is_home, far, out)
            err_out[a] = out[0, 0]

    def wait_sends():
        for g in range(slots - 1):
            @pl.when(sends_group(g))
            def _():
                all_of(row_x.at[0:128], group_send.at[g])
        for d in range(1, 8):
            @pl.when(sends_points(d))
            def _():
                point_copy(d).wait_send()
        all_of(sums_p.at[0:n_col - 1], sum_send.at[1])
        all_of(sums_z.at[0:n_row - 1], sum_send.at[0])
        all_of(bank.at[0:31], bank_send.at[0])
        for a in range(slots):
            @pl.when(q >= n_row * a + p)
            def _():
                pltpu.make_async_copy(wide.at[0:2], wide.at[0:2], zero_sem.at[a]).wait()

        @pl.when(is_home)
        def _():
            for c in help_copies:
                c().wait_send()
            pltpu.make_async_copy(wide.at[3], y_out.at[slots - 1], out_sem.at[0, 3]).wait()
            pltpu.make_async_copy(coef.at[3], c_out.at[slots - 1], out_sem.at[1, 3]).wait()

        @pl.when(is_helper)
        def _():
            for c in back_copies:
                c().wait_send()
        for k in range(3):
            @pl.when(job_off[k] & jnp.logical_not(is_helper) if k == 0 else job_off[k])
            def _():
                y_copy(k).wait()
                c_copy(k).wait()

    phase_enter()
    phase_setup()
    s_val = smooth[0]
    root = jnp.where(s_val >= 2, math.sqrt(5.0), jnp.where(s_val >= 1, math.sqrt(3.0), 1.0)).astype(F32)
    scale = (root * LOG2E) / jnp.full((8, LANES), reach[0], F32)
    linear = jnp.where(s_val >= 1, 1.0 / LOG2E, 0.0).astype(F32)
    square = jnp.where(s_val >= 2, 1.0 / (3.0 * LOG2E * LOG2E), 0.0).astype(F32)
    phase_barrier()
    phase_points()
    step_own()
    tile_part(0, 0)
    step_first(1)
    step_first(3)
    tile_part(0, 1)
    tile_part(0, 2)
    step_first(2)
    tile_part(0, 3)
    tile_part(1, 0)
    step_second(0)
    tile_part(1, 1)
    tile_part(1, 2)
    tile_part(1, 3)
    tile_part(2, 0)
    step_second(1)
    tile_part(2, 1)
    step_second(3)
    tile_part(2, 2)
    tile_part(2, 3)
    phase_share()
    step_second(2)
    send_z()
    wait_bank()
    products(0)
    send_y(0)
    phase_early()
    products(1)
    send_y(1)
    products(2)
    send_y(2)
    wait_z()
    phase_invert()
    send_p()
    phase_finish(0)
    phase_finish(1)
    phase_far_y()
    phase_finish(2)
    phase_far()
    total_error()
    wait_sends()


def solution(mesh):
    n_row, n_col = mesh.shape["prow"], mesh.shape["pcol"]

    def per_device(points, range_length, smoothness, sketch_bank, sketch_ids, tile_ranks):
        slots = sketch_ids.shape[0]
        nb = points.shape[3]
        rmax = sketch_bank.shape[1]
        dims = (slots, n_row, n_col, nb, rmax)
        anywhere = pl.BlockSpec(memory_space=pl.ANY)
        vmem = pltpu.VMEM
        hbm = pl.BlockSpec(memory_space=pltpu.HBM)
        scalars = pl.BlockSpec(memory_space=pltpu.SMEM)
        smem = pltpu.SMEM
        dma = pltpu.SemaphoreType.DMA
        y_out, c_out, err, rank = pl.pallas_call(
            functools.partial(kernel, dims),
            out_shape=(
                jax.ShapeDtypeStruct((slots, rmax, nb), F32),
                jax.ShapeDtypeStruct((slots, rmax, nb), F32),
                jax.ShapeDtypeStruct((slots,), F32),
                jax.ShapeDtypeStruct((1,), jnp.int32),
            ),
            in_specs=[hbm] * 6,
            out_specs=(anywhere, anywhere, scalars, scalars),
            scratch_shapes=[
                smem((1,), F32), smem((1,), jnp.int32), smem((slots,), jnp.int32), smem((slots,), jnp.int32),
                vmem((2, nb), F32), vmem((slots, 2, nb), F32), vmem((2, nb), F32),
                vmem((n_col, rmax, nb), BF16), vmem((3, nb, nb), BF16),
                vmem((nb, LANES), F32), vmem((nb, LANES), F32), vmem((8, nb), F32), vmem((8, nb), F32),
                vmem((3, nb, 3 * rmax), BF16), vmem((4, rmax, nb), F32), vmem((3, rmax, nb), F32),
                vmem((4, rmax, nb), F32), vmem((3, rmax, rmax), F32), vmem((nb, 3 * rmax), F32),
                vmem((3, 8, LANES), F32), vmem((3, 8, LANES), F32),
                vmem((rmax, nb), F32), vmem((8, LANES), jnp.int32), vmem((8, LANES), jnp.int32),
                vmem((rmax, nb), BF16), vmem((rmax, nb), BF16), vmem((rmax, nb), BF16), vmem((rmax, nb), BF16),
                vmem((8, LANES), F32), vmem((n_row, 8, LANES), F32), vmem((n_col, 8, LANES), F32),
                dma((6,)), dma((3,)), dma((8,)), dma((slots,)), dma((5,)), dma((5,)),
                dma((1,)), dma((4,)), dma((4,)), dma((1,)), dma((2,)), dma((2,)), dma((2, 4)), dma((slots,)),
            ],
            compiler_params=pltpu.CompilerParams(
                collective_id=0, has_side_effects=True, vmem_limit_bytes=VMEM_BYTES),
        )(
            points.reshape(2, nb), sketch_bank.reshape(rmax, nb), range_length, smoothness,
            sketch_ids.reshape(slots), tile_ranks.reshape(slots),
        )
        return (
            y_out.reshape(slots, 1, 1, 1, rmax, nb),
            c_out.reshape(slots, 1, 1, 1, rmax, nb),
            err.reshape(slots, 1, 1, 1),
            rank,
        )

    return jax.shard_map(
        per_device,
        mesh=mesh,
        in_specs=(
            P(None, "pcol", None, None),
            P(),
            P(),
            P("pcol", None, None),
            P(None, "prow", None, "pcol"),
            P(None, "prow", None, "pcol"),
        ),
        out_specs=(
            P(None, "prow", None, "pcol", None, None),
            P(None, "prow", None, "pcol", None, None),
            P(None, "prow", None, "pcol"),
            P(),
        ),
        check_vma=False,
    )
```

time: 286 us -> 48 us (0.17)
  the two profiles are of different devices: /device:TPU:1 before, /device:TPU:65 now
where the time goes in v2:
time: 48 us; the launch traced here: 47.8 us
  Pallas kernels  40.2 us (84%)
  local copies, waits for them, and re-layouts  3.81 us (8%)
  between operations  3.73 us (8%)
    pallas_call x1, Pallas kernels, per_device(): pl.pallas_call(functools.partial(kernel, dims), out_shape=(jax.ShapeDtype...  40.2 us
    unnamed x11, local copies, waits for them, and re-layouts  3.81 us

profile of v2, /device:TPU:65, one launch (start us, length us, event | category | flops | bytes accessed | tf_op | source)
XLA Modules:
  0.0 47.8 jit_solution(11322076256655096206)
XLA Ops:
  0.6 0.0 copy-start.1
  1.9 0.0 copy-start.2
  2.0 0.0 copy-start.3
  2.0 0.0 copy-done.1
  2.0 0.6 %copy-done.2 = s32[4,1,1,1]{0,3,2,1:T(1,128)S(1)} copy-done((s32[4,1,1,1]{0,3,2,1:T(1,128)S(1)}, s32[4,1,1,1]{0,3,2,1:T(1,128)}, u32[]{:S(2)}) %copy-start.2) | copy-done | bytes 40
  2.6 0.0 copy-done.3
  2.6 0.0 copy-start
  2.6 0.9 %copy-done = bf16[1,48,1024]{2,1,0:T(8,128)(2,1)S(1)} copy-done((bf16[1,48,1024]{2,1,0:T(8,128)(2,1)S(1)}, bf16[1,48,1024]{2,1,0:T(8,128)(2,1)}, u32[]{:S(2)}) %copy-start) | copy-done | bytes 98328
  3.5 40.2 %shard_map.93 = (f32[4,48,1024]{2,1,0:T(8,128)S(1)}, f32[4,48,1024]{2,1,0:T(8,128)S(1)}, f32[4]{0:T(128)S(1)}, s32[1]{0:T(128)}) custom-call(f32[2,1024]{1,0:T(2,128)S(1)} %bitcast.14, bf16[48,1024]{1,0:T(8,128)(2,1)S(1)} %bitcast.13, f32[1]{0:T(128)S(6)} %copy.16.reach_in, s32[1]{0:T(128)S(6)} %copy.17.smooth_in, s32[4]{0:T(128)S(1)} %bitcast.15, s32[4]{0:T(128)S(1)} %bitcast.16), custom_call_target="tpu_custom_call" | custom-call | tf_op jit(solution)/shard_map/pallas_call | solution.py:554
  43.8 0.9 %copy.18 = f32[4,1,1,1,48,1024]{5,4,3,2,1,0:T(8,128)} copy(f32[4,1,1,1,48,1024]{5,4,3,2,1,0:T(8,128)S(1)} %bitcast.12) | data formatting | bytes 1572864
  44.6 0.9 %copy.19 = f32[4,1,1,1,48,1024]{5,4,3,2,1,0:T(8,128)} copy(f32[4,1,1,1,48,1024]{5,4,3,2,1,0:T(8,128)S(1)} %bitcast.11) | data formatting | bytes 1572864
  45.5 0.5 %copy.20 = f32[4,1,1,1]{0,3,2,1:T(1,128)} copy(f32[4,1,1,1]{0,3,2,1:T(1,128)S(1)} %bitcast.17) | data formatting | bytes 32
Async XLA Ops:
  0.6 1.3 %copy-start.1 = (f32[1,1,2,1024]{3,2,1,0:T(2,128)S(1)}, f32[1,1,2,1024]{3,2,1,0:T(2,128)}, u32[]{:S(2)}) copy-start(f32[1,1,2,1024]{3,2,1,0:T(2,128)} %param.6) | copy-start | bytes 24580
  1.9 0.7 %copy-start.2 = (s32[4,1,1,1]{0,3,2,1:T(1,128)S(1)}, s32[4,1,1,1]{0,3,2,1:T(1,128)}, u32[]{:S(2)}) copy-start(s32[4,1,1,1]{0,3,2,1:T(1,128)} %param.10) | copy-start | bytes 52
  2.0 0.7 %copy-start.3 = (s32[4,1,1,1]{0,3,2,1:T(1,128)S(1)}, s32[4,1,1,1]{0,3,2,1:T(1,128)}, u32[]{:S(2)}) copy-start(s32[4,1,1,1]{0,3,2,1:T(1,128)} %param.11) | copy-start | bytes 52
  2.6 0.9 %copy-start = (bf16[1,48,1024]{2,1,0:T(8,128)(2,1)S(1)}, bf16[1,48,1024]{2,1,0:T(8,128)(2,1)}, u32[]{:S(2)}) copy-start(bf16[1,48,1024]{2,1,0:T(8,128)(2,1)} %param.9) | copy-start | bytes 294916

commit v3 on v2

v3 whole, which is shorter than its diff:
```python
import functools
import math

import jax
import jax.numpy as jnp
from jax import lax
from jax.experimental import pallas as pl
from jax.experimental.pallas import tpu as pltpu
from jax.sharding import PartitionSpec as P

MESH = pl.DeviceIdType.MESH
LOG2E = math.log2(math.e)
F32 = jnp.float32
BF16 = jnp.bfloat16
LANES = 128
VMEM_BYTES = 40 * 1024 * 1024
NT = (((1,), (1,)), ((), ()))


def kernel(dims, pts_in, sketch_in, ids_in, ranks_in, reach_in, smooth_in, y_out, c_out, err_out, rank_out,
           reach, smooth, ids, ranks, pts, rows, far_cols, bank, low, row_buf, col_x, col_y, left, wide, prod, coef, full, norms, errs,
           note, far_note, sent_y, sent_c, far_y, far_c, far_err, sums_z, sums_p,
           load_sem, group_send, pts_send, pts_recv, help_send, help_recv, bank_send, bank_recv1, bank_recv2, half_recv, mirror_recv,
           sum_send, sum_recv, out_sem):
    slots, n_row, n_col, nb, rmax = dims
    p = lax.axis_index("prow")
    q = lax.axis_index("pcol")
    y, x, core = q // 8, lax.rem(q // 2, 4), lax.rem(q, 2)
    partner = q + 1 - 2 * core
    is_home, is_helper = y == 0, y == slots - 1
    pair = lax.rem(q + (slots - 1) * n_row, n_col)
    job_slot = (jnp.where(is_home, 1, slots - 1), jnp.where(y == 2, 1, 2), y)
    job_on = (q >= 0, y <= 1, q <= n_row * y + p)
    job_off = (q >= 0, y <= 1, q < n_row * y + p)

    def remote(src, dst, send, recv, target):
        return pltpu.make_async_remote_copy(src, dst, send, recv, device_id={"pcol": target}, device_id_type=MESH)

    def all_of(ref, sem):
        pltpu.make_async_copy(ref, ref, sem).wait()

    def place(e, f):
        dy = core * e + (1 - core) * f
        dx = (1 - core) * e + core * f
        return lax.rem(y + dy + 8, 4) * 8 + lax.rem(x + dx + 8, 4) * 2 + core

    loads = [pltpu.make_async_copy(src, dst, load_sem.at[i]) for i, (src, dst) in enumerate((
        (ids_in, ids), (ranks_in, ranks), (smooth_in, smooth), (reach_in, reach), (pts_in, pts),
        (sketch_in, bank.at[q])))]
    barrier = pltpu.get_barrier_semaphore()

    def phase_enter():
        for load in loads:
            load.start()
        for d in range(1, n_col):
            pl.semaphore_signal(barrier, inc=1, device_id={"pcol": lax.rem(q + d, n_col)}, device_id_type=MESH)
        for d in range(1, n_row):
            pl.semaphore_signal(barrier, inc=1, device_id={"prow": lax.rem(p + d, n_row)}, device_id_type=MESH)

    lane = lax.broadcasted_iota(jnp.int32, (8, LANES), 1)
    sub = lax.broadcasted_iota(jnp.int32, (8, LANES), 0)

    def phase_setup():
        for load in loads:
            load.wait()
        note[...] = jnp.where(lane == 0, ids[slots - 1], ranks[slots - 1])
        wide[...] = jnp.zeros_like(wide)
        coef[...] = jnp.zeros_like(coef)
        norms[...] = jnp.zeros_like(norms)
        errs[...] = jnp.zeros_like(errs)

    mat_r = lax.broadcasted_iota(jnp.int32, (rmax, rmax), 0)
    mat_c = lax.broadcasted_iota(jnp.int32, (rmax, rmax), 1)
    eye = mat_r == mat_c

    def phase_barrier():
        pl.semaphore_wait(barrier, n_col - 1 + n_row - 1)

    is_source = lax.rem(q, n_row) == p

    def group_copy(g, i):
        return remote(pts, rows.at[y], group_send.at[g], pts_recv.at[y], g * 8 + i)

    def sends_group(g):
        return is_source & jnp.where(y == slots - 1, (g > 0) & (g < slots - 1), g < y)

    def point_copy(d):
        return remote(pts, rows.at[y], pts_send.at[d], pts_recv.at[y], y * 8 + lax.rem(q + d, 8))

    def sends_points(d):
        return is_source & ((y == slots - 1) | (lax.rem(q, 8) + d >= 8))

    help_copies = (
        lambda: remote(pts, far_cols, help_send.at[0], help_recv.at[0], pair),
        lambda: remote(note, far_note, help_send.at[1], help_recv.at[1], pair),
    )
    back = lax.rem(q + n_row, n_col)
    back_copies = (
        lambda: remote(sent_y, far_y, help_send.at[2], help_recv.at[2], back),
        lambda: remote(sent_c, far_c, help_send.at[3], help_recv.at[3], back),
        lambda: remote(errs.at[0], far_err, help_send.at[4], help_recv.at[4], back),
    )

    def phase_points():
        for g in range(slots - 1):
            @pl.when(sends_group(g))
            def _():
                for i in range(8):
                    group_copy(g, i).start()
        for d in range(1, 8):
            @pl.when(sends_points(d))
            def _():
                point_copy(d).start()

        @pl.when(is_home)
        def _():
            for c in help_copies:
                c().start()

    def first_copy(d):
        return remote(bank.at[q], bank.at[q], bank_send.at[0], bank_recv1.at[d], place(d, 0))

    def second_copy(e, d):
        block = place(-e, 0)
        return remote(bank.at[block], bank.at[block], bank_send.at[0], bank_recv2.at[e], place(0, d))

    def half_copy(e, d):
        block = place(-e, -d)
        cols = pl.ds(0 if d == 1 else nb // 2, nb // 2)
        return remote(bank.at[block, :, cols], bank.at[block, :, cols], bank_send.at[0], half_recv.at[e], place(0, d))

    def mirror_copy(e, f):
        block = place(-e, -f)
        return remote(bank.at[block], bank.at[block], bank_send.at[0], mirror_recv.at[0], partner)

    def ways(e):
        return (1, 3, 2) if e == 2 else (1, 3)

    def step_own():
        for d in (1, 3, 2):
            first_copy(d).start()
        for d in ways(0):
            second_copy(0, d).start()
        mirror_copy(0, 0).start()

    def step_first(e):
        first_copy(e).wait_recv()
        for d in ways(e):
            second_copy(e, d).start()
        mirror_copy(e, 0).start()

    def step_second(e):
        all_of(bank.at[0:len(ways(e))], bank_recv2.at[e])
        if e != 2:
            for d in (1, 3):
                half_copy(e, d).start()
        for d in ways(e):
            mirror_copy(e, d).start()

    def step_half(e):
        all_of(bank.at[0:1], half_recv.at[e])
        mirror_copy(e, 2).start()

    def prepare_rows(k, source):
        for cb in range(nb // LANES):
            cols = pl.ds(cb * LANES, LANES)
            for c in range(2):
                row_buf[k, c, cols, :] = jnp.broadcast_to(source[c:c + 1, cols] * scale[0:1, :], (LANES, LANES)).T

    def prepare_cols(source):
        for cb in range(nb // LANES):
            cols = pl.ds(cb * LANES, LANES)
            col_x[:, cols] = jnp.broadcast_to(source[0:1, cols], (8, LANES)) * scale
            col_y[:, cols] = jnp.broadcast_to(source[1:2, cols], (8, LANES)) * scale

    def generate(k, buf, g):
        acc = [jnp.zeros((8, LANES), F32) for _ in range(2)]
        for rg in range(LANES // 16):
            r = pl.multiple_of(g * LANES + rg * 16, 16)
            rx = row_buf[buf, 0, pl.ds(r, 16), :]
            ry = row_buf[buf, 1, pl.ds(r, 16), :]
            for cb in range(nb // LANES):
                cols = pl.ds(cb * LANES, LANES)
                cx, cy = col_x[:, cols], col_y[:, cols]
                tiles = []
                for h in range(2):
                    dx = rx[h * 8:h * 8 + 8] - cx
                    dy = ry[h * 8:h * 8 + 8] - cy
                    d2 = jnp.maximum(dx * dx + dy * dy, 1e-30)
                    t = d2 * lax.rsqrt(d2)
                    value = (1.0 + linear * t + square * d2) * jnp.exp2(-t)
                    acc[h] = acc[h] + value * value
                    tiles.append(value)
                low[k, pl.ds(r, 16), cols] = jnp.concatenate(tiles, 0).astype(BF16)
        norms[k] = norms[k] + (acc[0] + acc[1])

    def row_block(k, a):
        @pl.when(q == n_row * a + p)
        def _():
            prepare_rows(k, pts)

        @pl.when(q != n_row * a + p)
        def _():
            remote(pts, rows.at[a], pts_send.at[0], pts_recv.at[a], partner).wait_recv()
            prepare_rows(k, rows.at[a])

    job_rows = (0, 1, jnp.where(is_helper, 0, 2))

    def phase_rows(k):
        if k == 0:
            @pl.when(is_helper)
            def _():
                help_copies[0]().wait_recv()
                help_copies[1]().wait_recv()
                prepare_cols(far_cols)

            @pl.when(jnp.logical_not(is_helper))
            def _():
                prepare_cols(pts)
            for a in (1, slots - 1):
                @pl.when(job_slot[0] == a)
                def _():
                    row_block(0, a)
        if k == 1:
            @pl.when(job_on[1])
            def _():
                row_block(1, 2)
        if k == 2:
            for a in range(slots - 1):
                @pl.when((y == a) & job_on[2])
                def _():
                    row_block(2, a)

    def phase_cols():
        @pl.when(is_helper)
        def _():
            prepare_cols(pts)

    def tile(k, first, last):
        @pl.when(job_on[k])
        def _():
            def body(g, carry):
                generate(k, job_rows[k], g)
                return carry

            lax.fori_loop(first, last, body, 0)

    def z_copy(d):
        return pltpu.make_async_remote_copy(
            sums_z.at[p], sums_z.at[p], sum_send.at[0], sum_recv.at[0],
            device_id={"prow": lax.rem(p + d, n_row)}, device_id_type=MESH)

    def p_copy(d):
        return remote(sums_p.at[q], sums_p.at[q], sum_send.at[1], sum_recv.at[1], lax.rem(q + d, n_col))

    def phase_share():
        share = jnp.zeros((8, LANES), F32)
        for k in range(3):
            weight = jnp.where(job_off[k], 2.0, jnp.where(job_on[k], 1.0, 0.0)).astype(F32)
            share = share + weight * norms[k]
        rank_share = jnp.int32(0)
        for a in range(slots):
            rank_share = rank_share + jnp.where(q < n_row * a + p, ranks[a], 0)
        folded = jnp.sum(share, axis=0, keepdims=True)
        sums_z[p] = jnp.where(sub == 0, jnp.broadcast_to(folded, (8, LANES)),
                              jnp.where((sub == 1) & (lane == 0), rank_share.astype(F32), 0.0))

    def wait_bank():
        all_of(bank.at[0:16], mirror_recv.at[0])

    def send_z():
        for d in range(1, n_row):
            z_copy(d).start()

    y_copy = pltpu.make_async_copy(wide, y_out, out_sem.at[0])
    c_copy = pltpu.make_async_copy(coef, c_out, out_sem.at[1])

    def ranks_of(k):
        own = ranks[job_slot[k]]
        return jnp.where(is_helper, far_note[0:1, 1:2][0, 0], own) if k == 0 else own

    def id_of(k):
        own = ids[job_slot[k]]
        return jnp.where(is_helper, far_note[0:1, 0:1][0, 0], own) if k == 0 else own

    def project(k):
        rank = ranks_of(k)
        keep = lax.broadcasted_iota(jnp.int32, (rmax, nb), 0) < rank
        chosen = jnp.where(keep, bank[id_of(k)].astype(F32), 0.0).astype(BF16)
        sketched = lax.dot_general(chosen, low[k], NT, preferred_element_type=F32)
        high = sketched.astype(BF16)
        rest = sketched - high.astype(F32)
        middle = rest.astype(BF16)
        left[k] = jnp.concatenate([high, middle, (rest - middle.astype(F32)).astype(BF16)], 0)
        wide[job_slot[k]] = jnp.where(job_off[k], sketched, 0.0)

    def squares(k):
        @pl.when(job_off[k])
        def _():
            acc = [jnp.zeros((16, LANES), F32) for _ in range(4)]
            for r in range(0, nb, 16):
                for cb in range(nb // LANES):
                    value = low[k, r:r + 16, cb * LANES:(cb + 1) * LANES].astype(F32)
                    acc[cb % 4] = acc[cb % 4] + value * value
            acc = (acc[0] + acc[1]) + (acc[2] + acc[3])
            errs[k] = acc[:8] + acc[8:]

    def gram_of(k):
        both = lax.dot_general(left[k], left[k], NT, preferred_element_type=F32)
        both = both[2 * rmax:] + both[rmax:2 * rmax] + both[:rmax]
        return both[:, 2 * rmax:] + both[:, rmax:2 * rmax] + both[:, :rmax]

    def shifted(k, gram):
        rank = ranks_of(k)
        trace = jnp.sum(jnp.where(eye, gram, 0.0), keepdims=True)
        shift = 0.1 * trace / jnp.full((1, 1), rank.astype(F32))
        return gram + jnp.where(
            eye, jnp.where(mat_r < rank, jnp.broadcast_to(shift, (rmax, rmax)), 1.0), 0.0)

    def expand(k, n):
        cols = slice(n * 256, (n + 1) * 256)
        parts = jnp.dot(left[k], low[k, :, cols], preferred_element_type=F32)
        prod[k, :, cols] = parts[:rmax]
        full[k, :, cols] = parts[2 * rmax:] + parts[rmax:2 * rmax] + parts[:rmax]

    def times(a, b):
        a_high, b_high = a.astype(BF16), b.astype(BF16)
        a_low, b_low = (a - a_high.astype(F32)).astype(BF16), (b - b_high.astype(F32)).astype(BF16)
        return jnp.dot(jnp.concatenate([a_high, a_high, a_low], 1), jnp.concatenate([b_high, b_low, b_high], 0),
                       preferred_element_type=F32)

    def solve(jobs, grams):
        mats = [shifted(k, gram) for k, gram in zip(jobs, grams)]
        inverses = invert(mats, [functools.partial(expand, k, n) for k in jobs for n in range(nb // 256)])
        every = []
        for k, inverse in zip(jobs, inverses):
            coeffs = times(inverse, prod[k])
            coef[job_slot[k]] = jnp.where(job_off[k], coeffs, 0.0)
            every.append(coeffs)
            if jobs == (0,):
                sent_c[...] = coeffs.astype(BF16)
        for k, gram, coeffs in zip(jobs, grams, every):
            mixed = coeffs * (times(gram, coeffs) - 2.0 * full[k])
            acc = [jnp.zeros((8, LANES), F32) for _ in range(4)]
            for r in range(0, rmax, 8):
                for cb in range(nb // LANES):
                    acc[cb % 4] = acc[cb % 4] + mixed[r:r + 8, cb * LANES:(cb + 1) * LANES]
            errs[k] = errs[k] + ((acc[0] + acc[1]) + (acc[2] + acc[3]))

    def invert(mats, beside):
        mats = list(mats)
        b = 8
        row8 = lax.broadcasted_iota(jnp.int32, (b, rmax), 0)
        col8 = lax.broadcasted_iota(jnp.int32, (b, rmax), 1)
        for k0 in range(0, rmax, b):
            spread = [[[jnp.broadcast_to(m[i:i + b, k0 + j:k0 + j + 1], (b, rmax)) for j in range(b)]
                       for i in range(0, rmax, b)] for m in mats]
            for todo in beside[k0 // b * len(beside) * b // rmax:(k0 // b + 1) * len(beside) * b // rmax]:
                todo()
            for n in range(len(mats)):
                m = mats[n]
                d = list(spread[n][k0 // b])
                for j in range(b):
                    inverse = 1.0 / d[j][j:j + 1, :]
                    for i in range(b):
                        if i != j:
                            f = d[i][j:j + 1, :] * inverse
                            d[i] = jnp.where(row8 == j, f, d[i] - d[j] * f)
                    d[j] = jnp.where(row8 == j, inverse, -(d[j] * inverse))
                panel = m[k0:k0 + b]
                r = d[0] * panel[0:1]
                for j in range(1, b):
                    r = r + d[j] * panel[j:j + 1]
                for j in range(b):
                    r = jnp.where(col8 == k0 + j, d[j], r)
                inside = (col8 >= k0) & (col8 < k0 + b)
                out = []
                for i in range(0, rmax, b):
                    if i == k0:
                        out.append(r)
                        continue
                    piece = jnp.where(inside, 0.0, m[i:i + b])
                    for j in range(b):
                        piece = piece - spread[n][i // b][j] * r[j:j + 1]
                    out.append(piece)
                mats[n] = jnp.concatenate(out, 0)
        return mats

    def phase_project():
        @pl.when(jnp.logical_not(is_helper))
        def _():
            for k in range(3):
                project(k)

        @pl.when(is_helper)
        def _():
            project(0)
            sent_y[...] = left[0, :rmax]
            gram = gram_of(0)
            back_copies[0]().start()
            solve((0,), [gram])
            back_copies[1]().start()

    def phase_solve():
        @pl.when(jnp.logical_not(is_helper))
        def _():
            jobs = (0, 1, 2)
            grams = [gram_of(k) for k in jobs]
            solve(jobs, grams)

        @pl.when(is_helper)
        def _():
            back_copies[2]().start()
            project(2)
            gram = gram_of(2)
            solve((2,), [gram])

    def wait_z():
        all_of(sums_z.at[0:n_row - 1], sum_recv.at[0])
        plane = sums_z[0]
        for d in range(1, n_row):
            plane = plane + sums_z[d]
        sums_p[q] = plane

    def send_p():
        for d in range(1, n_col):
            p_copy(d).start()

    def phase_far_y():
        @pl.when(is_home)
        def _():
            back_copies[0]().wait_recv()
            wide[3] = far_y[...].astype(F32)
        y_copy.start()

    def phase_far():
        @pl.when(is_home)
        def _():
            for c in back_copies[1:]:
                c().wait_recv()
            coef[3] = far_c[...].astype(F32)
        c_copy.start()

    def total_error():
        all_of(sums_p.at[0:n_col - 1], sum_recv.at[1])
        whole = sums_p[0]
        for d in range(1, n_col):
            whole = whole + sums_p[d]
        total = jnp.sum(whole[0:1, :], keepdims=True)
        rank_out[0] = jnp.sum(whole[1:2, :]).astype(jnp.int32)
        factor = (n_row * slots) / jnp.sqrt(total)
        values = []
        for k in range(3):
            source = jnp.where(job_off[k], errs[k], norms[k])
            value = jnp.sqrt(jnp.maximum(jnp.sum(source, keepdims=True), 0.0)) * factor
            values.append(jnp.where(job_on[k], value, 0.0))
        far = jnp.sqrt(jnp.maximum(jnp.sum(far_err[...], keepdims=True), 0.0)) * factor
        for a in range(slots):
            out = jnp.zeros((1, 1), F32)
            for k in range(3):
                mine = (job_slot[k] == a) & job_on[k]
                if k == 0:
                    mine = mine & jnp.logical_not(is_helper)
                out = jnp.where(mine, values[k], out)
            if a == slots - 1:
                out = jnp.where(is_home, far, out)
            err_out[a] = out[0, 0]

    def wait_sends():
        for g in range(slots - 1):
            @pl.when(sends_group(g))
            def _():
                all_of(row_buf.at[0, 0, 0:LANES], group_send.at[g])
        for d in range(1, 8):
            @pl.when(sends_points(d))
            def _():
                point_copy(d).wait_send()
        all_of(sums_p.at[0:n_col - 1], sum_send.at[1])
        all_of(sums_z.at[0:n_row - 1], sum_send.at[0])
        all_of(bank.at[0:31], bank_send.at[0])

        @pl.when(is_home)
        def _():
            for c in help_copies:
                c().wait_send()

        @pl.when(is_helper)
        def _():
            for c in back_copies:
                c().wait_send()
        y_copy.wait()
        c_copy.wait()

    phase_enter()
    phase_setup()
    order = smooth[0]
    root = jnp.where(order >= 2, math.sqrt(5.0), jnp.where(order >= 1, math.sqrt(3.0), 1.0)).astype(F32)
    scale = (root * LOG2E) / jnp.full((8, LANES), reach[0], F32)
    linear = jnp.where(order >= 1, 1.0 / LOG2E, 0.0).astype(F32)
    square = jnp.where(order >= 2, 1.0 / (3.0 * LOG2E * LOG2E), 0.0).astype(F32)
    phase_barrier()
    phase_points()
    step_own()
    phase_rows(0)
    tile(0, 0, 2)
    step_first(1)
    step_first(3)
    phase_rows(1)
    phase_rows(2)
    tile(0, 2, 4)
    step_first(2)
    tile(0, 4, 8)
    step_second(0)
    tile(1, 0, 4)
    step_second(1)
    tile(1, 4, 8)
    phase_cols()
    step_second(3)
    step_half(0)
    tile(2, 0, 4)
    step_half(1)
    tile(2, 4, 8)
    phase_share()
    step_half(3)
    step_second(2)
    send_z()
    squares(0)
    squares(1)
    squares(2)
    wait_bank()
    phase_project()
    wait_z()
    send_p()
    phase_solve()
    phase_far_y()
    phase_far()
    total_error()
    wait_sends()


def solution(mesh):
    n_row, n_col = mesh.shape["prow"], mesh.shape["pcol"]

    def per_device(points, range_length, smoothness, sketch_bank, sketch_ids, tile_ranks):
        slots = sketch_ids.shape[0]
        nb = points.shape[3]
        rmax = sketch_bank.shape[1]
        dims = (slots, n_row, n_col, nb, rmax)
        anywhere = pl.BlockSpec(memory_space=pl.ANY)
        vmem = pltpu.VMEM
        hbm = pl.BlockSpec(memory_space=pltpu.HBM)
        scalars = pl.BlockSpec(memory_space=pltpu.SMEM)
        smem = pltpu.SMEM
        dma = pltpu.SemaphoreType.DMA
        y_out, c_out, err, rank = pl.pallas_call(
            functools.partial(kernel, dims),
            out_shape=(
                jax.ShapeDtypeStruct((slots, rmax, nb), F32),
                jax.ShapeDtypeStruct((slots, rmax, nb), F32),
                jax.ShapeDtypeStruct((slots,), F32),
                jax.ShapeDtypeStruct((1,), jnp.int32),
            ),
            in_specs=[hbm] * 6,
            out_specs=(anywhere, anywhere, scalars, scalars),
            scratch_shapes=[
                smem((1,), F32), smem((1,), jnp.int32), smem((slots,), jnp.int32), smem((slots,), jnp.int32),
                vmem((2, nb), F32), vmem((slots, 2, nb), F32), vmem((2, nb), F32),
                vmem((n_col, rmax, nb), BF16), vmem((3, nb, nb), BF16),
                vmem((3, 2, nb, LANES), F32), vmem((8, nb), F32), vmem((8, nb), F32),
                vmem((3, 3 * rmax, nb), BF16), vmem((4, rmax, nb), F32), vmem((3, rmax, nb), F32),
                vmem((4, rmax, nb), F32), vmem((3, rmax, nb), F32),
                vmem((3, 8, LANES), F32), vmem((3, 8, LANES), F32),
                vmem((8, LANES), jnp.int32), vmem((8, LANES), jnp.int32),
                vmem((rmax, nb), BF16), vmem((rmax, nb), BF16), vmem((rmax, nb), BF16), vmem((rmax, nb), BF16),
                vmem((8, LANES), F32), vmem((n_row, 8, LANES), F32), vmem((n_col, 8, LANES), F32),
                dma((6,)), dma((3,)), dma((8,)), dma((slots,)), dma((5,)), dma((5,)),
                dma((1,)), dma((4,)), dma((4,)), dma((4,)), dma((1,)), dma((2,)), dma((2,)), dma((2,)),
            ],
            compiler_params=pltpu.CompilerParams(
                collective_id=0, has_side_effects=True, vmem_limit_bytes=VMEM_BYTES),
        )(
            *(pltpu.with_memory_space_constraint(v, pltpu.HBM) for v in (
                points.reshape(2, nb), sketch_bank.reshape(rmax, nb),
                sketch_ids.reshape(slots), tile_ranks.reshape(slots))), range_length, smoothness,
        )
        return (
            y_out.reshape(slots, 1, 1, 1, rmax, nb),
            c_out.reshape(slots, 1, 1, 1, rmax, nb),
            err.reshape(slots, 1, 1, 1),
            rank,
        )

    return jax.shard_map(
        per_device,
        mesh=mesh,
        in_specs=(
            P(None, "pcol", None, None),
            P(),
            P(),
            P("pcol", None, None),
            P(None, "prow", None, "pcol"),
            P(None, "prow", None, "pcol"),
        ),
        out_specs=(
            P(None, "prow", None, "pcol", None, None),
            P(None, "prow", None, "pcol", None, None),
            P(None, "prow", None, "pcol"),
            P(),
        ),
        check_vma=False,
    )
```

time: 48 us -> 42.9 us (0.89)
  the two profiles are of different devices: /device:TPU:65 before, /device:TPU:1 now
where the time goes in v3:
time: 42.9 us; the launch traced here: 42.8 us
  Pallas kernels  36.9 us (86%)
  between operations  3.62 us (8%)
  local copies, waits for them, and re-layouts  2.27 us (5%)
    pallas_call x1, Pallas kernels, per_device(): pl.pallas_call(functools.partial(kernel, dims), out_shape=(jax.ShapeDtype...  36.9 us
    unnamed x3, local copies, waits for them, and re-layouts  2.27 us

profile of v3, /device:TPU:1, one launch (start us, length us, event | category | flops | bytes accessed | tf_op | source)
XLA Modules:
  0.0 42.8 jit_solution(17473719353664789499)
XLA Ops:
  1.9 36.9 %shard_map.93 = (f32[4,48,1024]{2,1,0:T(8,128)S(1)}, f32[4,48,1024]{2,1,0:T(8,128)S(1)}, f32[4]{0:T(128)S(1)}, s32[1]{0:T(128)}) custom-call(f32[2,1024]{1,0:T(2,128)} %bitcast.15, bf16[48,1024]{1,0:T(8,128)(2,1)} %bitcast.14, s32[4]{0:T(128)} %bitcast.16, s32[4]{0:T(128)} %bitcast.17, f32[1]{0:T(128)S(6)} %copy.16.reach_in, s32[1]{0:T(128)S(6)} %copy.17.smooth_in), custom_call_target="tpu_custom_call" | custom-call | tf_op jit(solution)/shard_map/pallas_call | solution.py:555
  38.8 0.9 %copy.18 = f32[4,1,1,1,48,1024]{5,4,3,2,1,0:T(8,128)} copy(f32[4,1,1,1,48,1024]{5,4,3,2,1,0:T(8,128)S(1)} %bitcast.12) | data formatting | bytes 1572864
  39.7 0.9 %copy.19 = f32[4,1,1,1,48,1024]{5,4,3,2,1,0:T(8,128)} copy(f32[4,1,1,1,48,1024]{5,4,3,2,1,0:T(8,128)S(1)} %bitcast.11) | data formatting | bytes 1572864
  40.6 0.5 %copy.20 = f32[4,1,1,1]{0,3,2,1:T(1,128)} copy(f32[4,1,1,1]{0,3,2,1:T(1,128)S(1)} %bitcast.13) | data formatting | bytes 32

commit v4 on v3

--- a/solution.py
+++ b/solution.py
@@ -27,11 +27,12 @@
     q = lax.axis_index("pcol")
     y, x, core = q // 8, lax.rem(q // 2, 4), lax.rem(q, 2)
     partner = q + 1 - 2 * core
-    is_home, is_helper = y == 0, y == slots - 1
+    turn = lax.rem(q, n_row)
+    is_home, is_helper = (y == 0) & (turn <= p), (y == slots - 1) & (turn <= p)
     pair = lax.rem(q + (slots - 1) * n_row, n_col)
-    job_slot = (jnp.where(is_home, 1, slots - 1), jnp.where(y == 2, 1, 2), y)
-    job_on = (q >= 0, y <= 1, q <= n_row * y + p)
-    job_off = (q >= 0, y <= 1, q < n_row * y + p)
+    job_slot = (jnp.where(y == 0, 1, slots - 1), jnp.where(y == 2, 1, 2), jnp.where((y == 0) & (turn > p), slots - 1, y))
+    job_on = ((y < slots - 1) | is_helper, y <= 1, (y == 0) | (turn <= p))
+    job_off = (job_on[0], job_on[1], job_on[2] & (turn != p))
 
     def remote(src, dst, send, recv, target):
         return pltpu.make_async_remote_copy(src, dst, send, recv, device_id={"pcol": target}, device_id_type=MESH)
@@ -64,15 +65,17 @@
         for load in loads:
             load.wait()
         note[...] = jnp.where(lane == 0, ids[slots - 1], ranks[slots - 1])
+
+    mat_r = lax.broadcasted_iota(jnp.int32, (rmax, rmax), 0)
+    mat_c = lax.broadcasted_iota(jnp.int32, (rmax, rmax), 1)
+    eye = mat_r == mat_c
+
+    def phase_clear():
         wide[...] = jnp.zeros_like(wide)
         coef[...] = jnp.zeros_like(coef)
         norms[...] = jnp.zeros_like(norms)
         errs[...] = jnp.zeros_like(errs)
 
-    mat_r = lax.broadcasted_iota(jnp.int32, (rmax, rmax), 0)
-    mat_c = lax.broadcasted_iota(jnp.int32, (rmax, rmax), 1)
-    eye = mat_r == mat_c
-
     def phase_barrier():
         pl.semaphore_wait(barrier, n_col - 1 + n_row - 1)
 
@@ -82,13 +85,13 @@
         return remote(pts, rows.at[y], group_send.at[g], pts_recv.at[y], g * 8 + i)
 
     def sends_group(g):
-        return is_source & jnp.where(y == slots - 1, (g > 0) & (g < slots - 1), g < y)
+        return is_source & (g < y)
 
     def point_copy(d):
         return remote(pts, rows.at[y], pts_send.at[d], pts_recv.at[y], y * 8 + lax.rem(q + d, 8))
 
     def sends_points(d):
-        return is_source & ((y == slots - 1) | (lax.rem(q, 8) + d >= 8))
+        return is_source & (turn + d >= 8)
 
     help_copies = (
         lambda: remote(pts, far_cols, help_send.at[0], help_recv.at[0], pair),
@@ -136,9 +139,12 @@
     def ways(e):
         return (1, 3, 2) if e == 2 else (1, 3)
 
+    def step_near():
+        for d in (1, 3):
+            first_copy(d).start()
+
     def step_own():
-        for d in (1, 3, 2):
-            first_copy(d).start()
+        first_copy(2).start()
         for d in ways(0):
             second_copy(0, d).start()
         mirror_copy(0, 0).start()
@@ -218,7 +224,7 @@
             def _():
                 prepare_cols(pts)
             for a in (1, slots - 1):
-                @pl.when(job_slot[0] == a)
+                @pl.when((job_slot[0] == a) & job_on[0])
                 def _():
                     row_block(0, a)
         if k == 1:
@@ -226,8 +232,8 @@
             def _():
                 row_block(1, 2)
         if k == 2:
-            for a in range(slots - 1):
-                @pl.when((y == a) & job_on[2])
+            for a in range(slots):
+                @pl.when((job_slot[2] == a) & job_on[2] & jnp.logical_not(is_helper))
                 def _():
                     row_block(2, a)
 
@@ -247,11 +253,11 @@
 
     def z_copy(d):
         return pltpu.make_async_remote_copy(
-            sums_z.at[p], sums_z.at[p], sum_send.at[0], sum_recv.at[0],
+            sums_z.at[p, 0:2], sums_z.at[p, 0:2], sum_send.at[0], sum_recv.at[0],
             device_id={"prow": lax.rem(p + d, n_row)}, device_id_type=MESH)
 
     def p_copy(d):
-        return remote(sums_p.at[q], sums_p.at[q], sum_send.at[1], sum_recv.at[1], lax.rem(q + d, n_col))
+        return remote(sums_p.at[q, 0:2], sums_p.at[q, 0:2], sum_send.at[1], sum_recv.at[1], lax.rem(q + d, n_col))
 
     def phase_share():
         share = jnp.zeros((8, LANES), F32)
@@ -287,23 +293,22 @@
         rank = ranks_of(k)
         keep = lax.broadcasted_iota(jnp.int32, (rmax, nb), 0) < rank
         chosen = jnp.where(keep, bank[id_of(k)].astype(F32), 0.0).astype(BF16)
-        sketched = lax.dot_general(chosen, low[k], NT, preferred_element_type=F32)
-        high = sketched.astype(BF16)
-        rest = sketched - high.astype(F32)
-        middle = rest.astype(BF16)
-        left[k] = jnp.concatenate([high, middle, (rest - middle.astype(F32)).astype(BF16)], 0)
-        wide[job_slot[k]] = jnp.where(job_off[k], sketched, 0.0)
-
-    def squares(k):
-        @pl.when(job_off[k])
-        def _():
-            acc = [jnp.zeros((16, LANES), F32) for _ in range(4)]
-            for r in range(0, nb, 16):
+        acc = [jnp.zeros((16, LANES), F32) for _ in range(4)]
+        width = 256
+        for n in range(nb // width):
+            cols = slice(n * width, (n + 1) * width)
+            sketched = lax.dot_general(chosen, low[k, cols, :], NT, preferred_element_type=F32)
+            high = sketched.astype(BF16)
+            rest = sketched - high.astype(F32)
+            middle = rest.astype(BF16)
+            left[k, :, cols] = jnp.concatenate([high, middle, (rest - middle.astype(F32)).astype(BF16)], 0)
+            wide[job_slot[k], :, cols] = jnp.where(job_off[k], sketched, 0.0)
+            for r in range(n * width, (n + 1) * width, 16):
                 for cb in range(nb // LANES):
                     value = low[k, r:r + 16, cb * LANES:(cb + 1) * LANES].astype(F32)
                     acc[cb % 4] = acc[cb % 4] + value * value
-            acc = (acc[0] + acc[1]) + (acc[2] + acc[3])
-            errs[k] = acc[:8] + acc[8:]
+        acc = (acc[0] + acc[1]) + (acc[2] + acc[3])
+        errs[k] = acc[:8] + acc[8:]
 
     def gram_of(k):
         both = lax.dot_general(left[k], left[k], NT, preferred_element_type=F32)
@@ -329,7 +334,7 @@
         return jnp.dot(jnp.concatenate([a_high, a_high, a_low], 1), jnp.concatenate([b_high, b_low, b_high], 0),
                        preferred_element_type=F32)
 
-    def solve(jobs, grams):
+    def solve(jobs, grams, ready=None):
         mats = [shifted(k, gram) for k, gram in zip(jobs, grams)]
         inverses = invert(mats, [functools.partial(expand, k, n) for k in jobs for n in range(nb // 256)])
         every = []
@@ -341,6 +346,8 @@
                 sent_c[...] = coeffs.astype(BF16)
         for k, gram, coeffs in zip(jobs, grams, every):
             mixed = coeffs * (times(gram, coeffs) - 2.0 * full[k])
+            if ready is not None:
+                ready()
             acc = [jnp.zeros((8, LANES), F32) for _ in range(4)]
             for r in range(0, rmax, 8):
                 for cb in range(nb // LANES):
@@ -398,8 +405,7 @@
             sent_y[...] = left[0, :rmax]
             gram = gram_of(0)
             back_copies[0]().start()
-            solve((0,), [gram])
-            back_copies[1]().start()
+            solve((0,), [gram], lambda: back_copies[1]().start())
 
     def phase_solve():
         @pl.when(jnp.logical_not(is_helper))
@@ -416,11 +422,11 @@
             solve((2,), [gram])
 
     def wait_z():
-        all_of(sums_z.at[0:n_row - 1], sum_recv.at[0])
-        plane = sums_z[0]
+        all_of(sums_z.at[0:n_row - 1, 0:2], sum_recv.at[0])
+        plane = sums_z[0, 0:2]
         for d in range(1, n_row):
-            plane = plane + sums_z[d]
-        sums_p[q] = plane
+            plane = plane + sums_z[d, 0:2]
+        sums_p[q, 0:2] = plane
 
     def send_p():
         for d in range(1, n_col):
@@ -442,10 +448,10 @@
         c_copy.start()
 
     def total_error():
-        all_of(sums_p.at[0:n_col - 1], sum_recv.at[1])
-        whole = sums_p[0]
+        all_of(sums_p.at[0:n_col - 1, 0:2], sum_recv.at[1])
+        whole = sums_p[0, 0:2]
         for d in range(1, n_col):
-            whole = whole + sums_p[d]
+            whole = whole + sums_p[d, 0:2]
         total = jnp.sum(whole[0:1, :], keepdims=True)
         rank_out[0] = jnp.sum(whole[1:2, :]).astype(jnp.int32)
         factor = (n_row * slots) / jnp.sqrt(total)
@@ -475,14 +481,15 @@
             @pl.when(sends_points(d))
             def _():
                 point_copy(d).wait_send()
-        all_of(sums_p.at[0:n_col - 1], sum_send.at[1])
-        all_of(sums_z.at[0:n_row - 1], sum_send.at[0])
+        all_of(sums_p.at[0:n_col - 1, 0:2], sum_send.at[1])
+        all_of(sums_z.at[0:n_row - 1, 0:2], sum_send.at[0])
         all_of(bank.at[0:31], bank_send.at[0])
 
         @pl.when(is_home)
         def _():
             for c in help_copies:
                 c().wait_send()
+            remote(pts, rows.at[slots - 1], pts_send.at[0], pts_recv.at[slots - 1], partner).wait_recv()
 
         @pl.when(is_helper)
         def _():
@@ -499,34 +506,36 @@
     linear = jnp.where(order >= 1, 1.0 / LOG2E, 0.0).astype(F32)
     square = jnp.where(order >= 2, 1.0 / (3.0 * LOG2E * LOG2E), 0.0).astype(F32)
     phase_barrier()
+    step_near()
     phase_points()
+    phase_clear()
     step_own()
+    step_first(1)
+    step_first(3)
     phase_rows(0)
     tile(0, 0, 2)
-    step_first(1)
-    step_first(3)
     phase_rows(1)
     phase_rows(2)
+    step_first(2)
     tile(0, 2, 4)
-    step_first(2)
+    step_second(0)
     tile(0, 4, 8)
-    step_second(0)
-    tile(1, 0, 4)
+    tile(1, 0, 2)
     step_second(1)
+    tile(1, 2, 4)
+    step_second(3)
     tile(1, 4, 8)
     phase_cols()
-    step_second(3)
+    tile(2, 0, 2)
     step_half(0)
-    tile(2, 0, 4)
+    step_second(2)
+    tile(2, 2, 4)
     step_half(1)
-    tile(2, 4, 8)
+    tile(2, 4, 6)
+    step_half(3)
+    tile(2, 6, 8)
     phase_share()
-    step_half(3)
-    step_second(2)
     send_z()
-    squares(0)
-    squares(1)
-    squares(2)
     wait_bank()
     phase_project()
     wait_z()

time: 42.9 us -> 41.4 us (0.965)
  Pallas kernels: 36.9 us -> 35.3 us
    pallas_call x1, Pallas kernels: 36.9 us -> 35.3 us  [per_device(): pl.pallas_call(functools.partial(kernel, dims), out_shape=(jax.ShapeDtype...]
where the time goes in v4:
time: 41.4 us; the launch traced here: 41.2 us
  Pallas kernels  35.3 us (85%)
  between operations  3.62 us (9%)
  local copies, waits for them, and re-layouts  2.27 us (5%)
    pallas_call x1, Pallas kernels, per_device(): pl.pallas_call(functools.partial(kernel, dims), out_shape=(jax.ShapeDtype...  35.3 us
    unnamed x3, local copies, waits for them, and re-layouts  2.27 us

profile of v4, /device:TPU:1, one launch (start us, length us, event | category | flops | bytes accessed | tf_op | source)
XLA Modules:
  0.0 41.2 jit_solution(10179222101835721919)
XLA Ops:
  1.9 35.3 %shard_map.93 = (f32[4,48,1024]{2,1,0:T(8,128)S(1)}, f32[4,48,1024]{2,1,0:T(8,128)S(1)}, f32[4]{0:T(128)S(1)}, s32[1]{0:T(128)}) custom-call(f32[2,1024]{1,0:T(2,128)} %bitcast.15, bf16[48,1024]{1,0:T(8,128)(2,1)} %bitcast.14, s32[4]{0:T(128)} %bitcast.16, s32[4]{0:T(128)} %bitcast.17, f32[1]{0:T(128)S(6)} %copy.16.reach_in, s32[1]{0:T(128)S(6)} %copy.17.smooth_in), custom_call_target="tpu_custom_call" | custom-call | tf_op jit(solution)/shard_map/pallas_call | solution.py:564
  37.2 0.9 %copy.18 = f32[4,1,1,1,48,1024]{5,4,3,2,1,0:T(8,128)} copy(f32[4,1,1,1,48,1024]{5,4,3,2,1,0:T(8,128)S(1)} %bitcast.12) | data formatting | bytes 1572864
  38.1 0.9 %copy.19 = f32[4,1,1,1,48,1024]{5,4,3,2,1,0:T(8,128)} copy(f32[4,1,1,1,48,1024]{5,4,3,2,1,0:T(8,128)S(1)} %bitcast.11) | data formatting | bytes 1572864
  39.0 0.5 %copy.20 = f32[4,1,1,1]{0,3,2,1:T(1,128)} copy(f32[4,1,1,1]{0,3,2,1:T(1,128)S(1)} %bitcast.13) | data formatting | bytes 32

commit v5 on v4

--- a/solution.py
+++ b/solution.py
@@ -18,7 +18,7 @@
 
 
 def kernel(dims, pts_in, sketch_in, ids_in, ranks_in, reach_in, smooth_in, y_out, c_out, err_out, rank_out,
-           reach, smooth, ids, ranks, pts, rows, far_cols, bank, low, row_buf, col_x, col_y, left, wide, prod, coef, full, norms, errs,
+           reach, smooth, ids, ranks, pts, rows, far_cols, bank, low, row_buf, col_x, col_y, left, wide, prod, coef, full, grams, norms, errs,
            note, far_note, sent_y, sent_c, far_y, far_c, far_err, sums_z, sums_p,
            load_sem, group_send, pts_send, pts_recv, help_send, help_recv, bank_send, bank_recv1, bank_recv2, half_recv, mirror_recv,
            sum_send, sum_recv, out_sem):
@@ -334,8 +334,12 @@
         return jnp.dot(jnp.concatenate([a_high, a_high, a_low], 1), jnp.concatenate([b_high, b_low, b_high], 0),
                        preferred_element_type=F32)
 
-    def solve(jobs, grams, ready=None):
-        mats = [shifted(k, gram) for k, gram in zip(jobs, grams)]
+    def keep_gram(k):
+        gram = gram_of(k)
+        grams[0, k] = gram
+        grams[1, k] = shifted(k, gram)
+
+    def solve(jobs, plain, mats, ready=None):
         inverses = invert(mats, [functools.partial(expand, k, n) for k in jobs for n in range(nb // 256)])
         every = []
         for k, inverse in zip(jobs, inverses):
@@ -344,7 +348,7 @@
             every.append(coeffs)
             if jobs == (0,):
                 sent_c[...] = coeffs.astype(BF16)
-        for k, gram, coeffs in zip(jobs, grams, every):
+        for k, gram, coeffs in zip(jobs, plain, every):
             mixed = coeffs * (times(gram, coeffs) - 2.0 * full[k])
             if ready is not None:
                 ready()
@@ -396,8 +400,12 @@
     def phase_project():
         @pl.when(jnp.logical_not(is_helper))
         def _():
-            for k in range(3):
-                project(k)
+            project(0)
+            project(1)
+            keep_gram(0)
+            project(2)
+            keep_gram(1)
+            keep_gram(2)
 
         @pl.when(is_helper)
         def _():
@@ -405,21 +413,20 @@
             sent_y[...] = left[0, :rmax]
             gram = gram_of(0)
             back_copies[0]().start()
-            solve((0,), [gram], lambda: back_copies[1]().start())
+            solve((0,), [gram], [shifted(0, gram)], lambda: back_copies[1]().start())
 
     def phase_solve():
         @pl.when(jnp.logical_not(is_helper))
         def _():
             jobs = (0, 1, 2)
-            grams = [gram_of(k) for k in jobs]
-            solve(jobs, grams)
+            solve(jobs, [grams[0, k] for k in jobs], [grams[1, k] for k in jobs])
 
         @pl.when(is_helper)
         def _():
             back_copies[2]().start()
             project(2)
             gram = gram_of(2)
-            solve((2,), [gram])
+            solve((2,), [gram], [shifted(2, gram)])
 
     def wait_z():
         all_of(sums_z.at[0:n_row - 1, 0:2], sum_recv.at[0])
@@ -506,14 +513,15 @@
     linear = jnp.where(order >= 1, 1.0 / LOG2E, 0.0).astype(F32)
     square = jnp.where(order >= 2, 1.0 / (3.0 * LOG2E * LOG2E), 0.0).astype(F32)
     phase_barrier()
+    phase_points()
     step_near()
-    phase_points()
     phase_clear()
     step_own()
+    phase_rows(0)
+    tile(0, 0, 1)
     step_first(1)
     step_first(3)
-    phase_rows(0)
-    tile(0, 0, 2)
+    tile(0, 1, 2)
     phase_rows(1)
     phase_rows(2)
     step_first(2)
@@ -577,7 +585,7 @@
                 vmem((n_col, rmax, nb), BF16), vmem((3, nb, nb), BF16),
                 vmem((3, 2, nb, LANES), F32), vmem((8, nb), F32), vmem((8, nb), F32),
                 vmem((3, 3 * rmax, nb), BF16), vmem((4, rmax, nb), F32), vmem((3, rmax, nb), F32),
-                vmem((4, rmax, nb), F32), vmem((3, rmax, nb), F32),
+                vmem((4, rmax, nb), F32), vmem((3, rmax, nb), F32), vmem((2, 3, rmax, rmax), F32),
                 vmem((3, 8, LANES), F32), vmem((3, 8, LANES), F32),
                 vmem((8, LANES), jnp.int32), vmem((8, LANES), jnp.int32),
                 vmem((rmax, nb), BF16), vmem((rmax, nb), BF16), vmem((rmax, nb), BF16), vmem((rmax, nb), BF16),

time: 41.4 us -> 41.4 us (level)
  no operation moved by 1% of the time
where the time goes in v5:
time: 41.4 us; the launch traced here: 41.2 us
  Pallas kernels  35.3 us (85%)
  between operations  3.62 us (9%)
  local copies, waits for them, and re-layouts  2.27 us (5%)
    pallas_call x1, Pallas kernels, per_device(): pl.pallas_call(functools.partial(kernel, dims), out_shape=(jax.ShapeDtype...  35.3 us
    unnamed x3, local copies, waits for them, and re-layouts  2.27 us

profile of v5, /device:TPU:1, one launch (start us, length us, event | category | flops | bytes accessed | tf_op | source)
XLA Modules:
  0.0 41.2 jit_solution(11974844296605273813)
XLA Ops:
  1.9 35.3 %shard_map.93 = (f32[4,48,1024]{2,1,0:T(8,128)S(1)}, f32[4,48,1024]{2,1,0:T(8,128)S(1)}, f32[4]{0:T(128)S(1)}, s32[1]{0:T(128)}) custom-call(f32[2,1024]{1,0:T(2,128)} %bitcast.15, bf16[48,1024]{1,0:T(8,128)(2,1)} %bitcast.14, s32[4]{0:T(128)} %bitcast.16, s32[4]{0:T(128)} %bitcast.17, f32[1]{0:T(128)S(6)} %copy.16.reach_in, s32[1]{0:T(128)S(6)} %copy.17.smooth_in), custom_call_target="tpu_custom_call" | custom-call | tf_op jit(solution)/shard_map/pallas_call | solution.py:572
  37.2 0.9 %copy.18 = f32[4,1,1,1,48,1024]{5,4,3,2,1,0:T(8,128)} copy(f32[4,1,1,1,48,1024]{5,4,3,2,1,0:T(8,128)S(1)} %bitcast.12) | data formatting | bytes 1572864
  38.1 0.9 %copy.19 = f32[4,1,1,1,48,1024]{5,4,3,2,1,0:T(8,128)} copy(f32[4,1,1,1,48,1024]{5,4,3,2,1,0:T(8,128)S(1)} %bitcast.11) | data formatting | bytes 1572864
  39.0 0.5 %copy.20 = f32[4,1,1,1]{0,3,2,1:T(1,128)} copy(f32[4,1,1,1]{0,3,2,1:T(1,128)S(1)} %bitcast.13) | data formatting | bytes 32
